TPU v7x, 256 devices: a whole 4x4x8 slice. The times are simulated.
256 devices in a mesh: ctx: 32 (over x, z_lo, core), tp: 8 (over z_hi, y).
Axes of the slice: x: 4, y: 4, z: 8 (z_hi: 2, z_lo: 4; z = z_hi * 4 + z_lo), core: 2. Of those that a mesh axis runs over, the one named last changes fastest.
Arguments:
- token_ids: int32 [24576], P('ctx'), may hold values from 0 to 511
- embed_table: bfloat16 [512, 4096], replicated, may hold values from -6 to 6
- norm_gain: float32 [4096], replicated, may hold values from 0.25 to 1.75
- w_in: bfloat16 [4096, 3, 2048], P(None, None, 'tp'), may hold values from -0.09375 to 0.09375
- short_taps: float32 [3, 3, 2048], P(None, None, 'tp'), may hold values from -3 to 3
- long_filter: bfloat16 [2048, 24576], P('tp', 'ctx'), may hold values from -0.0390625 to 0.0390625
- skip_gain: float32 [2048], P('tp'), may hold values from 0.5 to 2
- w_out: bfloat16 [2048, 4096], P(None, 'tp'), may hold values from -0.125 to 0.125
Outputs:
- mixed: bfloat16 [24576, 4096], P('ctx', 'tp')
All inputs are finite; a program needn't handle non-finite values.
Results may differ from a plain program's by a relative error of at most 0.0095.
Values may be sent and summed in bfloat16 or wider, within the bound.
A program may use at most 128 MiB of HBM per device.

v0:
```python
import math

import jax
import jax.numpy as jnp
from jax import lax
from jax.sharding import Mesh
from jax.sharding import PartitionSpec as P

CTX = ("ctx_0", "ctx_1", "ctx_2")


norm_eps = 1e-06


def shifted(block, axis, distance):
    devices = range(lax.axis_size(axis))
    route = [(i - distance, i) for i in devices if i - distance in devices]
    return lax.ppermute(block, axis, route)


def sent_together(arrays, axis, split_dim, concat_dim, along):
    ends, at = ([], 0)
    for a in arrays[:-1]:
        at += a.shape[along]
        ends.append(at)
    both = jnp.concatenate(arrays, axis=along)
    return tuple(
        jnp.split(
            lax.all_to_all(both, axis, split_axis=split_dim, concat_axis=concat_dim, tiled=True),
            ends,
            axis=along,
        )
    )


def in_blocks(x, dim, peers):
    dims = x.shape
    pieces = x.reshape(*dims[:dim], peers, dims[dim] // peers, *dims[dim + 1 :])
    return jnp.moveaxis(pieces, dim, 0)


def in_order(pieces, dim):
    dims = list(pieces.shape[1:])
    dims[dim] *= pieces.shape[0]
    return jnp.moveaxis(pieces, 0, dim).reshape(dims)


def turned_blocks(pieces, axes, sequence):
    inside = pieces.shape[1:]
    out = pieces.reshape(*(lax.axis_size(a) for a in axes), *inside)
    for k in sequence:
        out = lax.all_to_all(out, axes[k], k, k, tiled=True)
    return out.reshape(-1, *inside)


def core_and_chips(x, groups, sequence, split_dim, concat_dim):
    peers = lax.axis_size(groups[0]) * lax.axis_size(groups[1])
    pieces = in_blocks(x, split_dim, peers)
    return in_order(turned_blocks(pieces, groups, sequence), concat_dim)


def angle_table(outer, inner, period):
    product = (
        jnp.arange(outer, dtype=jnp.int32)[:, None]
        * jnp.arange(inner, dtype=jnp.int32)[None, :]
        % period
    )
    phase = product.astype(jnp.float32) * (2.0 * math.pi / period)
    return (jnp.cos(phase), jnp.sin(phase))


def contract(form, left, right):
    return jnp.einsum(form, left, right, preferred_element_type=jnp.float32)


def forward_transform(signal, tables):
    cos_rows, sin_rows, cos_twist, sin_twist, cos_cols, sin_cols = tables
    first_real = contract("kn,cnm->ckm", cos_rows, signal)
    first_imag = -contract("kn,cnm->ckm", sin_rows, signal)
    turned_real = first_real * cos_twist + first_imag * sin_twist
    turned_imag = first_imag * cos_twist - first_real * sin_twist
    spec_real = contract("ckm,mj->ckj", turned_real, cos_cols) + contract(
        "ckm,mj->ckj", turned_imag, sin_cols
    )
    spec_imag = contract("ckm,mj->ckj", turned_imag, cos_cols) - contract(
        "ckm,mj->ckj", turned_real, sin_cols
    )
    return (spec_real, spec_imag)


def inverse_transform(spec_real, spec_imag, tables, period):
    cos_rows, sin_rows, cos_twist, sin_twist, cos_cols, sin_cols = tables
    back_real = contract("ckj,mj->ckm", spec_real, cos_cols) - contract(
        "ckj,mj->ckm", spec_imag, sin_cols
    )
    back_imag = contract("ckj,mj->ckm", spec_imag, cos_cols) + contract(
        "ckj,mj->ckm", spec_real, sin_cols
    )
    untwist_real = back_real * cos_twist - back_imag * sin_twist
    untwist_imag = back_imag * cos_twist + back_real * sin_twist
    signal = contract("kn,ckm->cnm", cos_rows, untwist_real) - contract(
        "kn,ckm->cnm", sin_rows, untwist_imag
    )
    return signal / period


def causal_conv(signal, kernel):
    channels = signal.shape[0]
    length = signal.shape[1]
    col_count = min(256, length)
    row_count = 2 * length // col_count
    half_rows = length // col_count
    cos_rows, sin_rows = angle_table(row_count, half_rows, row_count)
    cos_twist, sin_twist = angle_table(row_count, col_count, row_count * col_count)
    cos_cols, sin_cols = angle_table(col_count, col_count, col_count)
    tables = (cos_rows, sin_rows, cos_twist, sin_twist, cos_cols, sin_cols)
    signal_real, signal_imag = forward_transform(
        signal.astype(jnp.float32).reshape(channels, half_rows, col_count), tables
    )
    kernel_real, kernel_imag = forward_transform(
        kernel.astype(jnp.float32).reshape(channels, half_rows, col_count), tables
    )
    joint_real = signal_real * kernel_real - signal_imag * kernel_imag
    joint_imag = signal_real * kernel_imag + signal_imag * kernel_real
    result = inverse_transform(joint_real, joint_imag, tables, row_count * col_count)
    return result.reshape(channels, length)


def local(token_ids, embed_table, norm_gain, w_in, short_taps, long_filter, skip_gain, w_out):
    vocab = embed_table.shape[0]
    one_hot = (token_ids[:, None] == jnp.arange(vocab, dtype=jnp.int32)[None, :]).astype(
        jnp.bfloat16
    )
    embedded = jnp.dot(one_hot, embed_table, preferred_element_type=jnp.float32)
    scale = lax.rsqrt(jnp.mean(embedded * embedded, axis=1, keepdims=True) + norm_eps)
    normed = (embedded * scale * norm_gain).astype(jnp.bfloat16)
    width = w_in.shape[0]
    chan_part = w_in.shape[2]
    flat_proj = jnp.dot(
        normed, w_in.reshape(width, 3 * chan_part), preferred_element_type=jnp.float32
    ).astype(jnp.bfloat16)
    projected = jnp.transpose(flat_proj.reshape(-1, 3, chan_part), (1, 2, 0))
    positions = projected.shape[2]
    edge = projected[:, :, positions - 2 :]
    prior = shifted(edge, CTX, 1)
    extended = jnp.concatenate([prior, projected], axis=2).astype(jnp.float32)
    shortened = (
        short_taps[0][:, :, None] * extended[:, :, 2:]
        + short_taps[1][:, :, None] * extended[:, :, 1 : positions + 1]
        + short_taps[2][:, :, None] * extended[:, :, 0:positions]
    ).astype(jnp.bfloat16)
    query_side = shortened[0]
    key_side = shortened[1]
    value_side = shortened[2]
    local_channels = shortened.shape[1]
    groups = lax.axis_size(CTX)
    owned = local_channels // groups

    def spread(array):
        return array.reshape(groups, owned, array.shape[-1])

    first_channel = lax.axis_index(CTX) * owned
    own_skip = lax.dynamic_slice_in_dim(skip_gain, first_channel, owned)[:, None]
    product_local = (key_side.astype(jnp.float32) * value_side.astype(jnp.float32)).astype(
        jnp.bfloat16
    )
    arrived = sent_together((spread(product_local), spread(long_filter)), CTX, 0, 2, 1)
    product = arrived[0].reshape(owned, -1)
    filter_full = arrived[1].reshape(owned, -1)
    convolved = causal_conv(product, filter_full)
    outgoing = (convolved + own_skip * product.astype(jnp.float32)).astype(jnp.bfloat16)
    returned = core_and_chips(
        outgoing.reshape(1, owned, -1), (("ctx_0", "ctx_1"), "ctx_2"), (1, 0), 2, 0
    )
    returned = returned.reshape(local_channels, positions)
    gated = (query_side.astype(jnp.float32) * returned.astype(jnp.float32)).astype(jnp.bfloat16)
    width_part = w_out.shape[1]
    projected_out = jnp.dot(
        lax.all_gather(gated, "tp", axis=0, tiled=True).T, w_out, preferred_element_type=jnp.float32
    )
    residual = lax.dynamic_slice_in_dim(embedded, lax.axis_index("tp") * width_part, width_part, 1)
    return (residual + projected_out).astype(jnp.bfloat16)


def solution(mesh):
    finer = Mesh(mesh.devices.reshape(4, 4, 2, mesh.shape["tp"]), ("ctx_0", "ctx_1", "ctx_2", "tp"))
    in_specs = (
        P(CTX),
        P(),
        P(),
        P(None, None, "tp"),
        P(None, None, "tp"),
        P("tp", CTX),
        P("tp"),
        P(None, "tp"),
    )
    out_specs = P(CTX, "tp")
    return jax.shard_map(local, mesh=finer, in_specs=in_specs, out_specs=out_specs, check_vma=False)
```

profile of v0, /device:TPU:8, one launch (start us, length us, event | category | flops | bytes accessed | tf_op | source)
XLA Modules:
  0.0 230.5 jit_solution(8118276754307388498)
XLA Ops:
  6.5 0.0 copy-start
  6.5 8.8 %multiply_reduce_fusion = (f32[768]{0:T(1024)S(1)}, f32[768,4096]{1,0:T(8,128)}) fusion(bf16[512,4096]{1,0:T(8,128)(2,1)} %param.9, s32[768]{0:T(1024)} %param.8), kind=kOutput, calls=%fused_computation.1 | convolution fusion | flops 3227909376 | bytes 16783360 | tf_op jit(solution)/shard_map/dot_general | solution.py:134
  15.4 0.0 copy-start.4
  15.4 8.7 %copy.32 = bf16[4096,3,256]{0,2,1:T(8,128)(2,1)} copy(bf16[4096,3,256]{2,0,1:T(8,128)(2,1)} %param.11) | data formatting | bytes 12582912 | tf_op args[3]
  24.0 0.0 copy-done.4
  24.0 0.0 copy-start.3
  24.0 11.0 %fusion.19 = bf16[768,768]{0,1:T(8,128)(2,1)S(1)} fusion(bf16[4096,768]{0,1:T(8,128)(2,1)} %bitcast.149, f32[768,4096]{1,0:T(8,128)} %get-tuple-element.13, f32[4096]{0:T(1024)S(1)} %copy-done.4, f32[768]{0:T(1024)S(1)} %add_rsqrt_fusion), kind=kOutput, calls=%fused_computation.36 | convolution fusion | flops 4841865216 | bytes 20073472 | tf_op jit(solution)/shard_map/dot_general | solution.py:139
  35.1 0.1 slice.40
  35.2 1.8 collective-permute-start
  37.0 0.0 copy-done.3
  37.0 1.0 collective-permute-done
  38.0 0.6 maximum_convert_fusion
  38.6 0.0 copy-start.2
  38.6 2.0 fusion.4
  40.6 0.0 copy-start.1
  40.7 1.1 copy-done.1
  41.7 0.1 fusion.37
  41.8 0.0 copy-done.2
  41.8 0.0 copy-start.5
  41.8 0.9 pad_maximum_fusion
  42.8 12.9 %all-to-all-start = ((bf16[32,16,768]{2,1,0:T(8,128)(2,1)}), bf16[32,16,768]{2,1,0:T(8,128)(2,1)S(1)}, u32[]{:S(2)}, u32[]{:S(2)}) async-start(bf16[32,16,768]{2,1,0:T(8,128)(2,1)} %pad_maximum_fusion), calls=%async_computation | async-start | bytes 1572864 | tf_op jit(solution)/shard_map/all_to_all | solution.py:29
  55.7 0.2 all-gather.2.cloned.1.call-start
  56.0 0.0 copy-done.5
  56.0 0.1 dynamic_slice.7
  56.1 0.8 fusion.84
  56.9 21.1 %all-to-all-done = bf16[32,16,768]{2,1,0:T(8,128)(2,1)S(1)} async-done(((bf16[32,16,768]{2,1,0:T(8,128)(2,1)}), bf16[32,16,768]{2,1,0:T(8,128)(2,1)S(1)}, u32[]{:S(2)}, u32[]{:S(2)}) %all-to-all-start) | async-done | bytes 786464 | tf_op jit(solution)/shard_map/all_to_all | solution.py:29
  77.9 0.1 copy.49
  78.0 0.1 fusion.204
  78.1 0.8 convolution_negate_fusion
  78.8 0.8 fusion.39
  79.6 0.8 convolution_negate_fusion.1
  80.4 0.8 fusion.42
  81.1 1.4 fusion.54
  82.5 1.4 fusion.58
  83.9 1.4 fusion.52
  85.3 1.4 fusion.48
  86.8 1.5 convolution_subtract_fusion.1
  88.2 1.4 convolution_add_fusion.2
  89.7 1.7 convolution_add_fusion.1
  91.3 1.8 multiply_add_fusion
  93.1 1.3 fusion.69
  94.4 1.3 fusion.71
  95.7 1.3 convolution_add_fusion
  97.0 1.3 convolution_subtract_fusion
  98.4 0.8 fusion.10
  99.1 1.7 fusion.26
  100.8 2.2 reshape.119
  103.0 1.6 fusion.31
  104.7 4.0 %all_to_all.28 = bf16[16,2,1,8,768]{4,3,0,2,1:T(8,128)(2,1)S(1)} all-to-all(bf16[16,2,1,8,768]{4,3,0,2,1:T(8,128)(2,1)S(1)} %copy.39), channel_id=1, replica_groups=mesh['ctx_0'=4,'ctx_1'=4,'ctx_2'=2,'tp'=8] {'ctx_2'}, dimensions={1} | all-to-all | bytes 786432 | tf_op jit(solution)/shard_map/all_to_all | solution.py:52
  108.7 17.4 %all_to_all.29 = bf16[16,2,1,8,768]{4,3,1,2,0:T(8,128)(2,1)S(1)} all-to-all(bf16[16,2,1,8,768]{4,3,1,2,0:T(8,128)(2,1)S(1)} %copy.40), channel_id=1, replica_groups=mesh['ctx_0'=4,'ctx_1'=4,'ctx_2'=2,'tp'=8] {'ctx_0','ctx_1'}, dimensions={0} | all-to-all | bytes 786432 | tf_op jit(solution)/shard_map/all_to_all | solution.py:52
  126.1 1.8 fusion.29
  127.9 0.0 all-gather.2.cloned.1.call-update
  128.0 90.6 %all-gather.2.cloned.1.call-done = bf16[2048,768]{1,0:T(8,128)(2,1)} async-done(((bf16[256,768]{1,0:T(8,128)(2,1)}), bf16[2048,768]{1,0:T(8,128)(2,1)}) %all-gather.2.cloned.1.call-update) | async-done | bytes 3145744 | tf_op jit(solution)/shard_map/all_gather | solution.py:179
  218.6 0.0 copy-done
  218.6 5.0 %add_convert_fusion = bf16[768,512]{1,0:T(8,128)(2,1)} fusion(f32[768,4096]{1,0:T(8,128)} %get-tuple-element.13, s32[]{:T(128)S(6)} %select_n.86, bf16[2048,768]{1,0:T(8,128)(2,1)} %all-gather.2.cloned.1.call-done, bf16[2048,512]{1,0:T(8,128)(2,1)S(1)} %copy-done), kind=kOutput, calls=%fused_computation.23 | convolution fusion | flops 1611399168 | bytes 7602180 | tf_op jit(solution)/shard_map/dot_general | solution.py:178
  (4 shorter events, 0.1 us)
Async XLA Ops:
  6.5 212.0 %copy-start = (bf16[2048,512]{1,0:T(8,128)(2,1)S(1)}, bf16[2048,512]{1,0:T(8,128)(2,1)}, u32[]{:S(2)}) copy-start(bf16[2048,512]{1,0:T(8,128)(2,1)} %param.15) | copy-start | bytes 6291460
  15.4 8.7 %copy-start.4 = (f32[4096]{0:T(1024)S(1)}, f32[4096]{0:T(1024)}, u32[]{:S(2)}) copy-start(f32[4096]{0:T(1024)} %param.10) | copy-start | bytes 49156
  24.0 12.9 %copy-start.3 = (f32[3,3,256]{2,1,0:T(4,128)S(1)}, f32[3,3,256]{2,1,0:T(4,128)}, u32[]{:S(2)}) copy-start(f32[3,3,256]{2,1,0:T(4,128)} %param.12) | copy-start | bytes 27652
  35.2 2.8 %collective-permute-start = (bf16[3,256,2]{2,1,0:T(8,128)(2,1)S(1)}, bf16[3,256,2]{2,1,0:T(8,128)(2,1)S(1)}, u32[]{:S(2)}, u32[]{:S(2)}) collective-permute-start(bf16[3,256,2]{2,1,0:T(8,128)(2,1)S(1)} %slice.40), channel_id=1, source_target_pairs={{0,8},{8,16},{16,24},{24,32},{32,40},{40,48},{48,56},{56,64},{64,7... | collective-permute-start | bytes 9224 | tf_op jit(solution)/shard_map/ppermute | solution.py:18
  38.6 3.2 %copy-start.2 = (bf16[256,768]{1,0:T(8,128)(2,1)S(1)}, bf16[256,768]{1,0:T(8,128)(2,1)}, u32[]{:S(2)}) copy-start(bf16[256,768]{1,0:T(8,128)(2,1)} %param.13) | copy-start | bytes 1179652
  40.6 1.1 copy-start.1
  41.8 14.1 %copy-start.5 = (f32[256]{0:T(256)S(1)}, f32[256]{0:T(256)}, u32[]{:S(2)}) copy-start(f32[256]{0:T(256)} %param.14) | copy-start | bytes 3076
  42.8 35.2 %all-to-all-start = ((bf16[32,16,768]{2,1,0:T(8,128)(2,1)}), bf16[32,16,768]{2,1,0:T(8,128)(2,1)S(1)}, u32[]{:S(2)}, u32[]{:S(2)}) async-start(bf16[32,16,768]{2,1,0:T(8,128)(2,1)} %pad_maximum_fusion), calls=%async_computation | async-start | bytes 1572864 | tf_op jit(solution)/shard_map/all_to_all | solution.py:29
  55.7 162.8 %all-gather.2.cloned.1.call-start = ((), (), s32[]{:S(2)}) async-start(), calls=%async_computation.3 | async-start | bytes 3538944 | tf_op jit(solution)/shard_map/all_gather | solution.py:179
Sparse Core Ops, SparseCore 0:
  128.1 90.4 all-gather.1
where the time goes:
time: 232 us; the launch traced here: 230 us
  waiting for transfers between devices  113 us (49%)
  matrix products  47.6 us (21%)
  blocking collectives  21.4 us (9%)
  starting transfers between devices  14.9 us (6%)
  between operations  13.6 us (6%)
  local copies, waits for them, and re-layouts  12.4 us (5%)
  other arithmetic  7.86 us (3%)
    all_gather x1, waiting for transfers between devices, local(): lax.all_gather(gated, 'tp', axis=0, tiled=True)  90.6 us
    dot_general x18, matrix products, contract(): return jnp.einsum(form, left, right, preferred_element_type=jnp.float32)  22.7 us
    all_to_all x2, blocking collectives, turned_blocks(): out = lax.all_to_all(out, axes[k], k, k, tiled=True)  21.4 us
    all_to_all x1, waiting for transfers between devices, sent_together(): lax.all_to_all(both, axis, split_axis=split_dim, concat_axis=concat_dim,...  21.1 us
    all_to_all x1, starting transfers between devices, sent_together(): lax.all_to_all(both, axis, split_axis=split_dim, concat_axis=concat_dim,...  12.9 us
    dot_general x1, matrix products, local(): jnp.dot(normed, w_in.reshape(width, 3 * chan_part), preferred_element_typ...  11 us
    unnamed x13, local copies, waits for them, and re-layouts  9.78 us
    dot_general x1, matrix products, local(): embedded = jnp.dot(one_hot, embed_table, preferred_element_type=jnp.float32)  8.82 us
  transfers between devices with their start and end apart: 3, of which 3 were waited for; matrix products, arithmetic and copies ran while one was open for 0% of the time, Pallas kernels for 0%

commit v1 on v0

v1 whole, which is shorter than its diff:
```python
import functools
import math

import jax
import jax.numpy as jnp
import numpy as np
from jax import lax
from jax.experimental import pallas as pl
from jax.experimental.pallas import tpu as pltpu
from jax.sharding import Mesh
from jax.sharding import PartitionSpec as P

CTX = ("x", "zl", "core")
MESH = pl.DeviceIdType.MESH
PEERS = 32
TP = 8
norm_eps = 1e-06


@functools.lru_cache(maxsize=None)
def tables(peers, per):
    R = peers * per
    N = 256 * R
    order = (np.arange(per)[:, None] + per * np.arange(peers)[None, :]).reshape(-1)
    k1 = np.arange(R) + 0.5
    a1 = 2 * np.pi * np.outer(k1, order) / (2 * R)
    f1 = np.concatenate([np.cos(a1), -np.sin(a1)], 0)
    at = 2 * np.pi * np.outer(k1, np.arange(128)) / N
    a2 = 2 * np.pi * (np.outer(np.arange(128), np.arange(128)) % 128) / 128
    c, s = np.cos(a2), np.sin(a2)
    w2 = np.block([[c, -s], [s, c]])
    w2i = np.block([[c, s], [-s, c]])
    f1i = np.concatenate([np.cos(a1.T), -np.sin(a1.T)], 1)
    return f1, np.cos(at), np.sin(at), w2, w2i, f1i


def peer_of(p):
    return {"x": p // 8, "zl": lax.rem(p // 2, 4), "core": lax.rem(p, 2)}


def ctx_index():
    return lax.axis_index("x") * 8 + lax.axis_index("zl") * 2 + lax.axis_index("core")


def exchange_kernel(count, *refs):
    ins, outs, ss, rs = refs[:count], refs[count : 2 * count], refs[2 * count], refs[2 * count + 1]
    me = ctx_index()
    bar = pltpu.get_barrier_semaphore()

    def greet(d, carry):
        pl.semaphore_signal(bar, inc=1, device_id=peer_of(lax.rem(me + d, PEERS)), device_id_type=MESH)
        return carry

    lax.fori_loop(1, PEERS, greet, 0)
    pl.semaphore_wait(bar, PEERS - 1)

    def copy(a, d):
        p = lax.rem(me + d, PEERS)
        return pltpu.make_async_remote_copy(
            src_ref=ins[a].at[p],
            dst_ref=outs[a].at[me],
            send_sem=ss.at[a, d],
            recv_sem=rs.at[a, d],
            device_id=peer_of(p),
            device_id_type=MESH,
        )

    for a in range(count):

        def go(d, carry, a=a):
            copy(a, d).start()
            return carry

        lax.fori_loop(1, PEERS, go, 0)
    for a in range(count):
        outs[a][me] = ins[a][me]

        def done(d, carry, a=a):
            copy(a, d).wait()
            return carry

        lax.fori_loop(1, PEERS, done, 0)


def exchange(arrays, cid):
    count = len(arrays)
    vmem = pl.BlockSpec(memory_space=pltpu.VMEM)
    return pl.pallas_call(
        functools.partial(exchange_kernel, count),
        out_shape=[jax.ShapeDtypeStruct(a.shape, a.dtype) for a in arrays],
        in_specs=[vmem] * count,
        out_specs=[vmem] * count,
        scratch_shapes=[
            pltpu.SemaphoreType.DMA((count, PEERS)),
            pltpu.SemaphoreType.DMA((count, PEERS)),
        ],
        compiler_params=pltpu.CompilerParams(collective_id=cid, has_side_effects=True),
        name=f"exchange_{cid}",
    )(*arrays)


def dot(a, b):
    return jnp.dot(a, b, preferred_element_type=jnp.float32)


def conv_kernel(x_ref, h_ref, gain_ref, f1_ref, ct_ref, st_ref, w2_ref, w2i_ref, f1i_ref, o_ref, flat, xs, spec, back, bs):
    peers, owned, span = x_ref.shape
    per = span // 128
    R = peers * per

    def forward(ref, slot):
        x = ref[...].astype(jnp.float32).reshape(peers * owned, span)
        for q in range(per):
            flat[q * peers * owned : (q + 1) * peers * owned, :] = x[:, q * 128 : (q + 1) * 128]
        for c in range(owned):
            for q in range(per):
                xs[q * peers : (q + 1) * peers, c * 128 : (c + 1) * 128] = flat[
                    pl.ds(q * peers * owned + c, peers, stride=owned), :
                ].astype(jnp.bfloat16)
        ct, st = ct_ref[...], st_ref[...]
        for c2 in range(owned // 2):
            first = dot(f1_ref[...], xs[:, c2 * 256 : (c2 + 1) * 256])
            for half in range(2):
                c = 2 * c2 + half
                re = first[:R, half * 128 : half * 128 + 128]
                im = first[R:, half * 128 : half * 128 + 128]
                rows = pl.ds(c * R, R)
                back[rows, 0:128] = (re * ct + im * st).astype(jnp.bfloat16)
                back[rows, 128:256] = (im * ct - re * st).astype(jnp.bfloat16)
        for c in range(owned):
            rows = pl.ds(c * R, R)
            spec[slot, rows, :] = dot(back[rows, :], w2_ref[...])

    forward(h_ref, 1)
    forward(x_ref, 0)
    ct, st = ct_ref[...], st_ref[...]
    for c in range(owned):
        rows = pl.ds(c * R, R)
        ar, ai = spec[0, rows, 0:128], spec[0, rows, 128:256]
        br, bi = spec[1, rows, 0:128], spec[1, rows, 128:256]
        back[rows, 0:128] = (ar * br - ai * bi).astype(jnp.bfloat16)
        back[rows, 128:256] = (ar * bi + ai * br).astype(jnp.bfloat16)
        u = dot(back[rows, :], w2i_ref[...])
        ur, ui = u[:, 0:128], u[:, 128:256]
        bs[0:R, c * 128 : (c + 1) * 128] = (ur * ct - ui * st).astype(jnp.bfloat16)
        bs[R : 2 * R, c * 128 : (c + 1) * 128] = (ui * ct + ur * st).astype(jnp.bfloat16)
    scale = 2.0 / (256 * R)
    for c2 in range(owned // 2):
        y = dot(f1i_ref[...], bs[:, c2 * 256 : (c2 + 1) * 256]) * scale
        for half in range(2):
            c = 2 * c2 + half
            for q in range(per):
                flat[pl.ds(q * peers * owned + c, peers, stride=owned), :] = y[
                    q * peers : (q + 1) * peers, half * 128 : half * 128 + 128
                ]
    for q in range(per):
        cols = slice(q * 128, (q + 1) * 128)
        x = x_ref[:, :, cols].astype(jnp.float32)
        y = flat[q * peers * owned : (q + 1) * peers * owned, :].reshape(peers, owned, 128)
        o_ref[:, :, cols] = (y + gain_ref[...] * x).astype(jnp.bfloat16)


def long_conv(x, h, gain):
    peers, owned, span = x.shape
    per = span // 128
    R = peers * per
    f1, ct, st, w2, w2i, f1i = tables(peers, per)
    bf = lambda a: jnp.asarray(a.astype(jnp.bfloat16))
    f32 = lambda a: jnp.asarray(a.astype(np.float32))
    vmem = pl.BlockSpec(memory_space=pltpu.VMEM)
    return pl.pallas_call(
        conv_kernel,
        out_shape=jax.ShapeDtypeStruct(x.shape, jnp.bfloat16),
        in_specs=[vmem] * 9,
        out_specs=vmem,
        scratch_shapes=[
            pltpu.VMEM((per * peers * owned, 128), jnp.float32),
            pltpu.VMEM((R, owned * 128), jnp.bfloat16),
            pltpu.VMEM((2, owned * R, 256), jnp.float32),
            pltpu.VMEM((owned * R, 256), jnp.bfloat16),
            pltpu.VMEM((2 * R, owned * 128), jnp.bfloat16),
        ],
        name="long_conv",
    )(x, h, gain, bf(f1), f32(ct), f32(st), bf(w2), bf(w2i), bf(f1i))


CHUNKS = 6


def output_kernel(g_ref, w_ref, res_ref, o_ref, buf, zs, zr, us, ur, ds, dr, ls, lr):
    zh, y = lax.axis_index("zh"), lax.axis_index("y")
    own, other = zh * 4 + y, (1 - zh) * 4 + y
    up, down = lax.rem(y + 1, 4), lax.rem(y + 3, 4)
    T = g_ref.shape[0]
    part = g_ref.shape[1]
    step = T // CHUNKS
    bar = pltpu.get_barrier_semaphore()
    for dev in ({"zh": 1 - zh}, {"y": up}, {"y": down}):
        pl.semaphore_signal(bar, inc=1, device_id=dev, device_id_type=MESH)
    pl.semaphore_wait(bar, 3)

    def send(src, dst, s, r, dev):
        return pltpu.make_async_remote_copy(
            src_ref=src, dst_ref=dst, send_sem=s, recv_sem=r, device_id=dev, device_id_type=MESH
        )

    def rows(c):
        return pl.ds(c * step, step)

    def across(c):
        return send(g_ref.at[rows(c)], buf.at[own, rows(c)], zs.at[c], zr.at[c], {"zh": 1 - zh})

    def slot(k, yy):
        return (zh if k == 0 else 1 - zh) * 4 + yy

    def direct(k, c, upward):
        src = g_ref.at[rows(c)] if k == 0 else buf.at[other, rows(c)]
        s, r = (us, ur) if upward else (ds, dr)
        return send(
            src, buf.at[slot(k, y), rows(c)], s.at[k, c], r.at[k, c], {"y": up if upward else down}
        )

    def relay(k, c):
        upward = c % 2 == 0
        b = slot(k, down if upward else up)
        return send(buf.at[b, rows(c)], buf.at[b, rows(c)], ls.at[k, c], lr.at[k, c], {"y": up if upward else down})

    def forward(k, c):
        upward = c % 2 == 0
        direct(k, c, upward).wait_recv()
        relay(k, c).start()

    def spread(c):
        across(c).wait_recv()
        direct(1, c, True).start()
        direct(1, c, False).start()

    for c in range(CHUNKS):
        across(c).start()
        direct(0, c, True).start()
        direct(0, c, False).start()
    buf[own] = g_ref[...]
    order = []
    for c in range(CHUNKS):
        order.append((forward, (0, c)))
        if c % 2 == 1:
            order.append((spread, ((c - 1) // 2,)))
    for c in range(CHUNKS // 2, CHUNKS):
        order.append((spread, (c,)))
        order.append((forward, (1, c - CHUNKS // 2)))
    for c in range(CHUNKS // 2, CHUNKS):
        order.append((forward, (1, c)))
    for f, a in order:
        f(*a)
    for c in range(CHUNKS):
        for k in range(2):
            direct(k, c, c % 2 == 1).wait_recv()
            relay(k, c).wait_recv()
        acc = res_ref[rows(c), :].astype(jnp.float32)
        for j in range(TP):
            acc += dot(buf[j, rows(c), :], w_ref[j * part : (j + 1) * part, :])
        o_ref[rows(c), :] = acc.astype(jnp.bfloat16)
    for c in range(CHUNKS):
        across(c).wait_send()
        for k in range(2):
            direct(k, c, True).wait_send()
            direct(k, c, False).wait_send()
            relay(k, c).wait_send()


def output(gated, w_out, residual, cid):
    T, part = gated.shape
    vmem = pl.BlockSpec(memory_space=pltpu.VMEM)
    dma = pltpu.SemaphoreType.DMA
    return pl.pallas_call(
        output_kernel,
        out_shape=jax.ShapeDtypeStruct(residual.shape, jnp.bfloat16),
        in_specs=[vmem] * 3,
        out_specs=vmem,
        scratch_shapes=[
            pltpu.VMEM((TP, T, part), jnp.bfloat16),
            dma((CHUNKS,)),
            dma((CHUNKS,)),
            dma((2, CHUNKS)),
            dma((2, CHUNKS)),
            dma((2, CHUNKS)),
            dma((2, CHUNKS)),
            dma((2, CHUNKS)),
            dma((2, CHUNKS)),
        ],
        compiler_params=pltpu.CompilerParams(collective_id=cid, has_side_effects=True),
        name="output",
    )(gated, w_out, residual)


def shifted(block, axis, distance):
    devices = range(lax.axis_size(axis))
    route = [(i - distance, i) for i in devices if i - distance in devices]
    return lax.ppermute(block, axis, route)


def local(token_ids, embed_table, norm_gain, w_in, short_taps, long_filter, skip_gain, w_out):
    vocab = embed_table.shape[0]
    T = token_ids.shape[0]
    chan = w_in.shape[2]
    owned = chan // PEERS
    prior = shifted(token_ids[T - 2 :] + 1, CTX, 1)
    ids = jnp.concatenate([prior, token_ids + 1]) - 1
    table = embed_table.astype(jnp.float32)
    scale = lax.rsqrt(jnp.mean(table * table, axis=1, keepdims=True) + norm_eps)
    normed = (table * scale * norm_gain).astype(jnp.bfloat16)
    w3 = jnp.transpose(w_in, (1, 0, 2))
    rows = [dot(normed, w3[s]).astype(jnp.bfloat16) for s in range(3)]
    hot = (ids[:, None] == jnp.arange(vocab, dtype=jnp.int32)[None, :]).astype(jnp.bfloat16)
    residual = dot(
        hot[2:], lax.dynamic_slice_in_dim(embed_table, (lax.axis_index("zh") * 4 + lax.axis_index("y")) * w_out.shape[1], w_out.shape[1], 1)
    ).astype(jnp.bfloat16)

    def short(s):
        e = lax.dot_general(rows[s], hot, (((0,), (1,)), ((), ())), preferred_element_type=jnp.float32)
        return (
            short_taps[0, s][:, None] * e[:, 2:]
            + short_taps[1, s][:, None] * e[:, 1 : T + 1]
            + short_taps[2, s][:, None] * e[:, 0:T]
        ).astype(jnp.bfloat16)

    query, key, value = short(0), short(1), short(2)
    product = (key.astype(jnp.float32) * value.astype(jnp.float32)).astype(jnp.bfloat16)
    px, ph = exchange([product.reshape(PEERS, owned, T), long_filter.reshape(PEERS, owned, T)], 0)
    own_skip = lax.dynamic_slice_in_dim(skip_gain, ctx_index() * owned, owned)[:, None]
    skipped = long_conv(px, ph, own_skip)
    (returned,) = exchange([skipped], 1)
    returned = returned.reshape(chan, T)
    gated = (query.astype(jnp.float32) * returned.astype(jnp.float32)).astype(jnp.bfloat16).T
    return output(gated, w_out, residual, 2)


def solution(mesh):
    finer = Mesh(mesh.devices.reshape(4, 4, 2, 2, 4), ("x", "zl", "core", "zh", "y"))
    tp = ("zh", "y")
    in_specs = (
        P(CTX),
        P(),
        P(),
        P(None, None, tp),
        P(None, None, tp),
        P(tp, CTX),
        P(tp),
        P(None, tp),
    )
    return jax.shard_map(local, mesh=finer, in_specs=in_specs, out_specs=P(CTX, tp), check_vma=False)
```

time: 232 us -> 122 us (0.53)
  waiting for transfers between devices: 113 us -> 0.01 us
  Pallas kernels: 0 us -> 88.8 us
  matrix products: 47.6 us -> 17.1 us
  blocking collectives: 21.4 us -> 0 us
  between operations: 13.6 us -> 0.1 us
  starting transfers between devices: 14.9 us -> 1.73 us
  local copies, waits for them, and re-layouts: 12.4 us -> 4.85 us
    all_gather x1 -> x0, waiting for transfers between devices: 90.6 us -> none  [local(): lax.all_gather(gated, 'tp', axis=0, tiled=True)]
    pallas_call x0 -> x4, Pallas kernels: none -> 88.8 us  [the longest x2 45 us: exchange(): pl.pallas_call(functools.partial(exchange_kernel, count), out_shape=[jax....]
    dot_general x21 -> x4, matrix products: 47.6 us -> 17.1 us  [the longest x3 14.6 us: short(): lax.dot_general(rows[s], hot, (((0,), (1,)), ((), ())), preferred_element...]
    all_to_all x2 -> x0, blocking collectives: 21.4 us -> none  [turned_blocks(): out = lax.all_to_all(out, axes[k], k, k, tiled=True)]
    all_to_all x1 -> x0, waiting for transfers between devices: 21.1 us -> none  [sent_together(): lax.all_to_all(both, axis, split_axis=split_dim, concat_axis=concat_dim,...]
    all_to_all x1 -> x0, starting transfers between devices: 12.9 us -> none  [sent_together(): lax.all_to_all(both, axis, split_axis=split_dim, concat_axis=concat_dim,...]
    unnamed x13 -> x5, local copies, waits for them, and re-layouts: 9.78 us -> 2.07 us
    convert_element_type x5 -> x2, other arithmetic: 6.11 us -> 1.56 us  [the longest x1 1.05 us: local(): returned.astype(jnp.float32)]
  transfers between devices with their start and end apart: 3 -> 1, of which waited for: 3 -> 0; matrix products, arithmetic and copies ran while one was open for 0% -> 4% of each run, Pallas kernels for 0% -> 0%
where the time goes in v1:
time: 122 us; the launch traced here: 120 us
  Pallas kernels  88.8 us (73%)
  matrix products  17.1 us (14%)
  other arithmetic  7.5 us (6%)
  local copies, waits for them, and re-layouts  4.85 us (4%)
  starting transfers between devices  1.73 us (1%)
    pallas_call x2, Pallas kernels, exchange(): pl.pallas_call(functools.partial(exchange_kernel, count), out_shape=[jax....  45 us
    pallas_call x1, Pallas kernels, output(): pl.pallas_call(output_kernel, out_shape=jax.ShapeDtypeStruct(residual.sha...  39.6 us
    dot_general x3, matrix products, short(): lax.dot_general(rows[s], hot, (((0,), (1,)), ((), ())), preferred_element...  14.6 us
    pallas_call x1, Pallas kernels, long_conv(): pl.pallas_call(conv_kernel, out_shape=jax.ShapeDtypeStruct(x.shape, jnp.b...  4.26 us
    reduce_sum x1, other arithmetic, local(): scale = lax.rsqrt(jnp.mean(table * table, axis=1, keepdims=True) + norm_eps)  3.08 us
    dot_general x1, matrix products, dot(): return jnp.dot(a, b, preferred_element_type=jnp.float32)  2.52 us
  transfers between devices with their start and end apart: 1, of which 0 were waited for; matrix products, arithmetic and copies ran while one was open for 4% of the time, Pallas kernels for 0%

profile of v1, /device:TPU:8, one launch (start us, length us, event | category | flops | bytes accessed | tf_op | source)
XLA Modules:
  0.0 120.1 jit_solution(3769306359319868777)
XLA Ops:
  0.0 0.0 copy-start
  0.0 0.0 copy-start.1
  0.0 0.8 slice_add_fusion
  0.8 1.7 %collective-permute-start = (s32[2]{0:T(128)S(1)}, s32[2]{0:T(128)S(1)}, u32[]{:S(2)}, u32[]{:S(2)}) collective-permute-start(s32[2]{0:T(128)S(1)} %slice_add_fusion), channel_id=1, source_target_pairs={{0,8},{8,16},{16,24},{24,32},{32,40},{40,48},{48,56},{56,64},{64,7... | collective-permute-start | bytes 32 | tf_op jit(solution)/shard_map/ppermute | solution.py:299
  2.5 0.7 broadcast_add_fusion
  3.2 0.8 fusion.38
  4.1 3.1 %fusion = f32[512]{0:T(512)S(1)} fusion(bf16[512,4096]{1,0:T(8,128)(2,1)} %param.15), kind=kLoop, calls=%fused_computation.2 | loop fusion | flops 6290944 | bytes 4196352 | tf_op jit(solution)/shard_map/reduce_sum | solution.py:310
  7.2 0.0 copy-done
  7.2 0.1 dynamic-slice_bitcast_fusion
  7.3 0.7 copy.19.gain_ref
  7.9 0.0 collective-permute-done
  7.9 0.1 add_add_fusion
  8.0 0.0 copy-done.1
  8.0 4.8 %fusion.11 = f32[256,770]{0,1:T(8,128)S(1)} fusion(bf16[3,4096,256]{2,1,0:T(8,128)(2,1)} %bitcast.51, s32[770]{0:T(1024)S(1)} %add_add_fusion, bf16[512,4096]{1,0:T(8,128)(2,1)} %param.15, f32[4096]{0:T(1024)S(1)} %copy-done.1, f32[512]{0:T(512)S(1)} %add_rsqrt_fusion), kind=kOutput, calls=%fused_computation.15 | convolution fusion | flops 1284506624 | bytes 7101448 | tf_op jit(solution)/shard_map/dot_general | solution.py:320
  12.9 4.9 %fusion.12 = f32[256,770]{0,1:T(8,128)S(1)} fusion(bf16[3,4096,256]{2,1,0:T(8,128)(2,1)} %bitcast.52, s32[770]{0:T(1024)S(1)} %add_add_fusion, bf16[512,4096]{1,0:T(8,128)(2,1)} %param.15, f32[4096]{0:T(1024)S(1)} %copy-done.1, f32[512]{0:T(512)S(1)} %add_rsqrt_fusion), kind=kOutput, calls=%fused_computation.16 | convolution fusion | flops 1284506624 | bytes 7101448 | tf_op jit(solution)/shard_map/dot_general | solution.py:320
  17.7 4.9 %fusion.13 = f32[256,770]{0,1:T(8,128)S(1)} fusion(bf16[3,4096,256]{2,1,0:T(8,128)(2,1)} %bitcast.53, s32[770]{0:T(1024)S(1)} %add_add_fusion, bf16[512,4096]{1,0:T(8,128)(2,1)} %param.15, f32[4096]{0:T(1024)S(1)} %copy-done.1, f32[512]{0:T(512)S(1)} %add_rsqrt_fusion), kind=kOutput, calls=%fused_computation.17 | convolution fusion | flops 1284506624 | bytes 7101448 | tf_op jit(solution)/shard_map/dot_general | solution.py:320
  22.6 0.3 iota_compare_fusion
  22.9 0.5 multiply_convert_fusion.1
  23.4 0.9 copy.18
  24.3 28.7 %exchange_0.1 = (bf16[32,8,768]{2,1,0:T(8,128)(2,1)}, bf16[32,8,768]{2,1,0:T(8,128)(2,1)}) custom-call(bf16[32,8,768]{2,1,0:T(8,128)(2,1)} %bitcast.40, bf16[32,8,768]{2,1,0:T(8,128)(2,1)} %bitcast.41), custom_call_target="tpu_custom_call" | custom-call | tf_op jit(solution)/shard_map/exchange_0/pallas_call | solution.py:88
  53.0 4.3 %long_conv.1.refs_0_ = bf16[32,8,768]{2,1,0:T(8,128)(2,1)} custom-call(bf16[32,8,768]{2,1,0:T(8,128)(2,1)} %get-tuple-element.7.x_ref, bf16[32,8,768]{2,1,0:T(8,128)(2,1)} %get-tuple-element.8.h_ref, f32[8,1]{1,0:T(8,128)} %copy.19.gain_ref, bf16[384,192]{1,0:T(8,128)(2,1)} %constant.59.clone.f1_ref, f32[192,128]{1,0:T(8,128)} %constant.60.clone.ct_ref, ...), custom_call_target="tpu_custom_call" | custom-call | tf_op jit(solution)/shard_map/long_conv/pallas_call | solution.py:171
  57.2 16.3 %exchange_1.1 = bf16[32,8,768]{2,1,0:T(8,128)(2,1)} custom-call(bf16[32,8,768]{2,1,0:T(8,128)(2,1)} %long_conv.1.refs_0_), custom_call_target="tpu_custom_call" | custom-call | tf_op jit(solution)/shard_map/exchange_1/pallas_call | solution.py:88
  73.5 1.0 bitcast_convert_fusion
  74.6 0.3 copy.20
  74.9 2.5 %fusion.8.res_ref = bf16[768,512]{1,0:T(8,128)(2,1)} fusion(pred[770,512]{1,0:T(8,128)(4,1)S(1)} %iota_compare_fusion, bf16[512,4096]{1,0:T(8,128)(2,1)} %param.15, s32[]{:T(128)S(6)} %select_n.7), kind=kOutput, calls=%fused_computation.14 | convolution fusion | flops 403046400 | bytes 1703940 | tf_op jit(solution)/shard_map/dot_general | solution.py:103
  77.4 1.0 fusion.30.g_ref
  78.4 39.6 %output.1 = bf16[768,512]{1,0:T(8,128)(2,1)} custom-call(bf16[768,256]{1,0:T(8,128)(2,1)} %fusion.30.g_ref, bf16[2048,512]{1,0:T(8,128)(2,1)} %w_ref.1, bf16[768,512]{1,0:T(8,128)(2,1)} %fusion.8.res_ref), custom_call_target="tpu_custom_call" | custom-call | tf_op jit(solution)/shard_map/output/pallas_call | solution.py:275
  118.0 2.1 %copy.22 = bf16[768,512]{1,0:T(8,128)(2,1)} copy(bf16[768,512]{1,0:T(8,128)(2,1)} %output.1) | data formatting | bytes 1572864
  (1 shorter events, 0.0 us)
Async XLA Ops:
  0.0 7.2 %copy-start = (f32[256]{0:T(256)S(1)}, f32[256]{0:T(256)}, u32[]{:S(2)}) copy-start(f32[256]{0:T(256)} %param.20) | copy-start | bytes 3076
  0.0 8.0 %copy-start.1 = (f32[4096]{0:T(1024)S(1)}, f32[4096]{0:T(1024)}, u32[]{:S(2)}) copy-start(f32[4096]{0:T(1024)} %param.16) | copy-start | bytes 49156
  0.8 7.1 %collective-permute-start = (s32[2]{0:T(128)S(1)}, s32[2]{0:T(128)S(1)}, u32[]{:S(2)}, u32[]{:S(2)}) collective-permute-start(s32[2]{0:T(128)S(1)} %slice_add_fusion), channel_id=1, source_target_pairs={{0,8},{8,16},{16,24},{24,32},{32,40},{40,48},{48,56},{56,64},{64,7... | collective-permute-start | bytes 32 | tf_op jit(solution)/shard_map/ppermute | solution.py:299

commit v2 on v1

v2 whole, which is shorter than its diff:
```python
import functools
import math

import jax
import jax.numpy as jnp
import numpy as np
from jax import lax
from jax.experimental import pallas as pl
from jax.experimental.pallas import tpu as pltpu
from jax.sharding import Mesh
from jax.sharding import PartitionSpec as P

CTX = ("x", "zl", "core")
MESH = pl.DeviceIdType.MESH
PEERS = 32
TP = 8
norm_eps = 1e-06


@functools.lru_cache(maxsize=None)
def tables(peers, per):
    R = peers * per
    N = 256 * R
    order = (np.arange(per)[:, None] + per * np.arange(peers)[None, :]).reshape(-1)
    k1 = np.arange(R) + 0.5
    a1 = 2 * np.pi * np.outer(k1, order) / (2 * R)
    f1 = np.concatenate([np.cos(a1), -np.sin(a1)], 0)
    at = 2 * np.pi * np.outer(k1, np.arange(128)) / N
    a2 = 2 * np.pi * (np.outer(np.arange(128), np.arange(128)) % 128) / 128
    c, s = np.cos(a2), np.sin(a2)
    w2 = np.block([[c, -s], [s, c]])
    w2i = np.block([[c, s], [-s, c]])
    f1i = np.concatenate([np.cos(a1.T), -np.sin(a1.T)], 1)
    return f1, np.cos(at), np.sin(at), w2, w2i, f1i


def peer_of(p):
    return {"x": p // 8, "zl": lax.rem(p // 2, 4), "core": lax.rem(p, 2)}


def ctx_index():
    return lax.axis_index("x") * 8 + lax.axis_index("zl") * 2 + lax.axis_index("core")


def dot(a, b):
    return jnp.dot(a, b, preferred_element_type=jnp.float32)


def send(src, dst, s, r, dev):
    return pltpu.make_async_remote_copy(
        src_ref=src, dst_ref=dst, send_sem=s, recv_sem=r, device_id=dev, device_id_type=MESH
    )


CHUNKS = 6
HALO = 16


def normalize(tv, gain_ref, nv):
    vocab, width = tv.shape

    @pl.loop(0, vocab // 32)
    def _(r):
        rows = pl.ds(pl.multiple_of(r * 32, 32), 32)
        acc = jnp.zeros((32, 128), jnp.float32)
        for j in range(width // 128):
            x = tv[rows, j * 128 : (j + 1) * 128].astype(jnp.float32)
            acc += x * x
        scale = lax.rsqrt(jnp.sum(acc, axis=1, keepdims=True) * (1.0 / width) + norm_eps)
        for j in range(width // 128):
            cols = slice(j * 128, (j + 1) * 128)
            x = tv[rows, cols].astype(jnp.float32)
            nv[rows, cols] = (x * scale * gain_ref[:, cols]).astype(jnp.bfloat16)


def one_hot(ids_row, vocab):
    column = jnp.transpose(jnp.broadcast_to(ids_row, (128, 128)))
    lane = lax.broadcasted_iota(jnp.int32, (128, 128), 1)
    return [(column == lane + 128 * j) for j in range(vocab // 128)]


def block_kernel(
    ids_ref, gain_ref, taps_ref, skip_ref, ct_ref, st_ref, table_hbm, w3_hbm, filt_hbm, wo_hbm, f1_hbm, w2_hbm, w2i_hbm, f1i_hbm,
    o_ref,
    tv, nv, wv, pv, hot, ev, wo, f1, w2, w2i, f1i, idp, skips, qv, psend, px, hx, res, flat, xs, spec, back, bs, sk, ret, gv, buf,
    ld, ids_s, ids_r, fs, fr, ps, pr, xsnd, xrcv, zs, zr, us, ur, ds, dr, ls, lr,
):
    me = ctx_index()
    zh, y = lax.axis_index("zh"), lax.axis_index("y")
    own, other = zh * 4 + y, (1 - zh) * 4 + y
    up, down = lax.rem(y + 1, 4), lax.rem(y + 3, 4)
    vocab = tv.shape[0]
    T, part = qv.shape
    owned = part // PEERS
    step = T // CHUNKS
    per = T // 128
    R = PEERS * per

    loads = [
        pltpu.make_async_copy(a, b, ld.at[i])
        for i, (a, b) in enumerate(
            [
                (table_hbm, tv),
                (w3_hbm.at[0], wv.at[0]),
                (w3_hbm.at[1], wv.at[1]),
                (w3_hbm.at[2], wv.at[2]),
                (filt_hbm.at[me], hx.at[me]),
                (f1_hbm, f1),
                (w2_hbm, w2),
                (w2i_hbm, w2i),
                (f1i_hbm, f1i),
                (wo_hbm, wo),
            ]
        )
    ]
    for c in loads:
        c.start()

    bar = pltpu.get_barrier_semaphore()
    for dev in ({"zh": 1 - zh}, {"y": up}, {"y": down}):
        pl.semaphore_signal(bar, inc=1, device_id=dev, device_id_type=MESH)

    def greet(d, carry):
        pl.semaphore_signal(bar, inc=1, device_id=peer_of(lax.rem(me + d, PEERS)), device_id_type=MESH)
        return carry

    lax.fori_loop(1, PEERS, greet, 0)
    pl.semaphore_wait(bar, PEERS + 2)

    def to_all(make):
        def go(d, carry):
            make(lax.rem(me + d, PEERS)).start()
            return carry

        lax.fori_loop(1, PEERS, go, 0)

    nxt = lax.rem(me + 1, PEERS)
    ids_copy = send(ids_ref, idp, ids_s, ids_r, peer_of(nxt))
    ids_copy.start()
    to_all(lambda p: send(filt_hbm.at[p], hx.at[me], fs, fr, peer_of(p)))

    def all_of(ref, s, r):
        most = ref.at[pl.ds(0, PEERS - 1)]
        return send(most, most, s, r, peer_of(nxt))

    loads[0].wait()
    normalize(tv, gain_ref, nv)
    for s in range(3):
        loads[1 + s].wait()

    @pl.loop(0, 3)
    def _(s):
        pv[s] = dot(nv[...], wv[s]).astype(jnp.bfloat16)

    for b in range(per):
        for j, hit in enumerate(one_hot(ids_ref[b : b + 1, :], vocab)):
            hot[HALO + b * 128 : HALO + (b + 1) * 128, j * 128 : (j + 1) * 128] = hit.astype(jnp.float32).astype(jnp.bfloat16)
    ids_copy.wait_recv()
    for j, hit in enumerate(one_hot(idp[per - 1 : per, :], vocab)):
        keep = jnp.where(me > 0, hit[128 - HALO :, :].astype(jnp.float32), 0.0)
        hot[0:HALO, j * 128 : (j + 1) * 128] = keep.astype(jnp.bfloat16)
    for s in range(3):
        ev[:, s * part : (s + 1) * part] = dot(hot[...], pv[s])

    def short(s, b):
        cols = slice(s * part, (s + 1) * part)
        at = HALO + b * 128
        out = taps_ref[0, s : s + 1, :] * ev[at : at + 128, cols]
        out += taps_ref[1, s : s + 1, :] * ev[at - 1 : at + 127, cols]
        out += taps_ref[2, s : s + 1, :] * ev[at - 2 : at + 126, cols]
        return out.astype(jnp.bfloat16)

    for b in range(per):
        cols = slice(b * 128, (b + 1) * 128)
        key, value = short(1, b).astype(jnp.float32), short(2, b).astype(jnp.float32)
        psend[:, :, cols] = jnp.transpose(key * value).reshape(PEERS, owned, 128).astype(jnp.bfloat16)
    to_all(lambda p: send(psend.at[p], px.at[me], ps, pr, peer_of(p)))
    px[me] = psend[me]

    for b in range(per):
        qv[b * 128 : (b + 1) * 128, :] = short(0, b)
    width = o_ref.shape[1]
    res[...] = dot(hot[HALO:, :], tv[:, pl.ds(pl.multiple_of(own * width, width), width)]).astype(jnp.bfloat16)
    for j in range(part // 128):
        skips[j * 128 : (j + 1) * 128, :] = jnp.transpose(jnp.broadcast_to(skip_ref[j : j + 1, :], (128, 128)))

    def forward(ref, slot):
        for q in range(per):
            flat[q * PEERS * owned : (q + 1) * PEERS * owned, :] = ref[:, :, q * 128 : (q + 1) * 128].astype(jnp.float32).reshape(PEERS * owned, 128)
        for c in range(owned):
            for q in range(per):
                xs[q * PEERS : (q + 1) * PEERS, c * 128 : (c + 1) * 128] = flat[
                    pl.ds(q * PEERS * owned + c, PEERS, stride=owned), :
                ].astype(jnp.bfloat16)
        ct, st = ct_ref[...], st_ref[...]
        for c2 in range(owned // 2):
            first = dot(f1[...], xs[:, c2 * 256 : (c2 + 1) * 256])
            for half in range(2):
                c = 2 * c2 + half
                re = first[:R, half * 128 : half * 128 + 128]
                im = first[R:, half * 128 : half * 128 + 128]
                rows = slice(c * R, (c + 1) * R)
                back[rows, 0:128] = (re * ct + im * st).astype(jnp.bfloat16)
                back[rows, 128:256] = (im * ct - re * st).astype(jnp.bfloat16)
        for c in range(owned):
            rows = slice(c * R, (c + 1) * R)
            spec[slot, rows, :] = dot(back[rows, :], w2[...])

    for i in range(4, 9):
        loads[i].wait()
    all_of(hx, fs, fr).wait_recv()
    forward(hx, 1)
    all_of(px, ps, pr).wait_recv()
    forward(px, 0)
    ct, st = ct_ref[...], st_ref[...]
    for c in range(owned):
        rows = slice(c * R, (c + 1) * R)
        ar, ai = spec[0, rows, 0:128], spec[0, rows, 128:256]
        br, bi = spec[1, rows, 0:128], spec[1, rows, 128:256]
        back[rows, 0:128] = (ar * br - ai * bi).astype(jnp.bfloat16)
        back[rows, 128:256] = (ar * bi + ai * br).astype(jnp.bfloat16)
        u = dot(back[rows, :], w2i[...])
        ur_, ui_ = u[:, 0:128], u[:, 128:256]
        bs[0:R, c * 128 : (c + 1) * 128] = (ur_ * ct - ui_ * st).astype(jnp.bfloat16)
        bs[R : 2 * R, c * 128 : (c + 1) * 128] = (ui_ * ct + ur_ * st).astype(jnp.bfloat16)
    scale = 2.0 / (256 * R)
    for c2 in range(owned // 2):
        z = dot(f1i[...], bs[:, c2 * 256 : (c2 + 1) * 256]) * scale
        for half in range(2):
            c = 2 * c2 + half
            for q in range(per):
                flat[pl.ds(q * PEERS * owned + c, PEERS, stride=owned), :] = z[
                    q * PEERS : (q + 1) * PEERS, half * 128 : half * 128 + 128
                ]
    direct_gain = skips[pl.ds(pl.multiple_of(me * owned, owned), owned), :]
    for q in range(per):
        cols = slice(q * 128, (q + 1) * 128)
        x = px[:, :, cols].astype(jnp.float32)
        z = flat[q * PEERS * owned : (q + 1) * PEERS * owned, :].reshape(PEERS, owned, 128)
        sk[:, :, cols] = (z + direct_gain[None] * x).astype(jnp.bfloat16)

    def cols_of(q):
        return pl.ds(q * step, step)

    def across(c):
        return send(gv.at[cols_of(c)], buf.at[own, cols_of(c)], zs.at[c], zr.at[c], {"zh": 1 - zh})

    def slot_of(k, yy):
        return (zh if k == 0 else 1 - zh) * 4 + yy

    def direct(k, c, upward):
        src = gv.at[cols_of(c)] if k == 0 else buf.at[other, cols_of(c)]
        s, r = (us, ur) if upward else (ds, dr)
        return send(
            src, buf.at[slot_of(k, y), cols_of(c)], s.at[k, c], r.at[k, c], {"y": up if upward else down}
        )

    def relay(k, c):
        upward = c % 2 == 0
        b = slot_of(k, down if upward else up)
        here = buf.at[b, cols_of(c)]
        return send(here, here, ls.at[k, c], lr.at[k, c], {"y": up if upward else down})

    def returned(q):
        most = ret.at[pl.ds(0, PEERS - 1), :, cols_of(q)]
        return send(most, most, xsnd.at[q], xrcv.at[q], peer_of(nxt))

    def gate(q):
        rows = slice(q * step, (q + 1) * step)
        returned(q).wait_recv()
        arrived = jnp.transpose(ret[:, :, rows].astype(jnp.float32).reshape(part, step))
        gated = (arrived * qv[rows, :].astype(jnp.float32)).astype(jnp.bfloat16)
        gv[rows, :] = gated
        across(q).start()
        direct(0, q, True).start()
        direct(0, q, False).start()
        buf[own, rows, :] = gated

    def pass_on(k, c):
        direct(k, c, c % 2 == 0).wait_recv()
        relay(k, c).start()

    def spread(c):
        across(c).wait_recv()
        direct(1, c, True).start()
        direct(1, c, False).start()

    def finish(c):
        rows = slice(c * step, (c + 1) * step)
        for k in range(2):
            direct(k, c, c % 2 == 1).wait_recv()
            relay(k, c).wait_recv()
        acc = res[rows, :].astype(jnp.float32)
        for j in range(TP):
            acc += dot(buf[j, rows, :], wo[j * part : (j + 1) * part, :])
        o_ref[rows, :] = acc.astype(jnp.bfloat16)

    for q in range(CHUNKS):
        to_all(lambda p: send(sk.at[p, :, cols_of(q)], ret.at[me, :, cols_of(q)], xsnd.at[q], xrcv.at[q], peer_of(p)))
    ret[me] = sk[me]
    loads[9].wait()
    for s in range(CHUNKS + 5):
        for f, lag in ((gate, 0), (lambda c: pass_on(0, c), 1), (spread, 2), (lambda c: pass_on(1, c), 3), (finish, 4)):
            if 0 <= s - lag < CHUNKS:
                f(s - lag)

    ids_copy.wait_send()
    all_of(hx, fs, fr).wait_send()
    all_of(px, ps, pr).wait_send()
    for c in range(CHUNKS):
        returned(c).wait_send()
        across(c).wait_send()
        for k in range(2):
            direct(k, c, True).wait_send()
            direct(k, c, False).wait_send()
            relay(k, c).wait_send()


def local(token_ids, embed_table, norm_gain, w_in, short_taps, long_filter, skip_gain, w_out):
    vocab, width = embed_table.shape
    T = token_ids.shape[0]
    part = w_in.shape[2]
    owned = part // PEERS
    per = T // 128
    R = PEERS * per
    cols = w_out.shape[1]
    f1, ct, st, w2, w2i, f1i = tables(PEERS, per)
    bf = lambda a: jnp.asarray(a.astype(jnp.bfloat16))
    f32 = lambda a: jnp.asarray(a.astype(np.float32))
    vmem = pl.BlockSpec(memory_space=pltpu.VMEM)
    hbm = pl.BlockSpec(memory_space=pl.ANY)
    dma = pltpu.SemaphoreType.DMA
    B, F = jnp.bfloat16, jnp.float32
    V = pltpu.VMEM
    return pl.pallas_call(
        block_kernel,
        out_shape=jax.ShapeDtypeStruct((T, cols), B),
        in_specs=[vmem] * 6 + [hbm] * 8,
        out_specs=vmem,
        scratch_shapes=[
            V((vocab, width), B),
            V((vocab, width), B),
            V((3, width, part), B),
            V((3, vocab, part), B),
            V((HALO + T, vocab), B),
            V((HALO + T, 3 * part), F),
            V(w_out.shape, B),
            V(f1.shape, B),
            V(w2.shape, B),
            V(w2i.shape, B),
            V(f1i.shape, B),
            V((per, 128), jnp.int32),
            V((part, 128), F),
            V((T, part), B),
            V((PEERS, owned, T), B),
            V((PEERS, owned, T), B),
            V((PEERS, owned, T), B),
            V((T, cols), B),
            V((per * part, 128), F),
            V((R, owned * 128), B),
            V((2, owned * R, 256), F),
            V((owned * R, 256), B),
            V((2 * R, owned * 128), B),
            V((PEERS, owned, T), B),
            V((PEERS, owned, T), B),
            V((T, part), B),
            V((TP, T, part), B),
            dma((10,)),
            dma,
            dma,
            dma,
            dma,
            dma,
            dma,
            dma((CHUNKS,)),
            dma((CHUNKS,)),
            dma((CHUNKS,)),
            dma((CHUNKS,)),
        ]
        + [dma((2, CHUNKS))] * 6,
        compiler_params=pltpu.CompilerParams(collective_id=0, has_side_effects=True, vmem_limit_bytes=60 * 2**20),
        name="block",
    )(
        token_ids.reshape(per, 128),
        norm_gain.reshape(1, width),
        short_taps,
        skip_gain.reshape(part // 128, 128),
        f32(ct),
        f32(st),
        embed_table,
        jnp.transpose(w_in, (1, 0, 2)),
        long_filter.reshape(PEERS, owned, T),
        w_out,
        bf(f1),
        bf(w2),
        bf(w2i),
        bf(f1i),
    )


def solution(mesh):
    finer = Mesh(mesh.devices.reshape(4, 4, 2, 2, 4), ("x", "zl", "core", "zh", "y"))
    tp = ("zh", "y")
    in_specs = (
        P(CTX),
        P(),
        P(),
        P(None, None, tp),
        P(None, None, tp),
        P(tp, CTX),
        P(tp),
        P(None, tp),
    )
    return jax.shard_map(local, mesh=finer, in_specs=in_specs, out_specs=P(CTX, tp), check_vma=False)
```

time: 122 us -> 77.3 us (0.63); the launches traced: 120 us -> 77.2 us
  matrix products: 17.1 us -> 0 us
  Pallas kernels: 88.8 us -> 75.1 us
  other arithmetic: 7.5 us -> 0 us
  local copies, waits for them, and re-layouts: 4.85 us -> 2.06 us
  starting transfers between devices: 1.73 us -> 0 us
    dot_general x4 -> x0, matrix products: 17.1 us -> none  [the longest x3 14.6 us: short(): lax.dot_general(rows[s], hot, (((0,), (1,)), ((), ())), preferred_element...]
    pallas_call x4 -> x1, Pallas kernels: 88.8 us -> 75.1 us  [local(): pl.pallas_call(block_kernel, out_shape=jax.ShapeDtypeStruct((T, cols), B)...]
    reduce_sum x1 -> x0, other arithmetic: 3.08 us -> none  [local(): scale = lax.rsqrt(jnp.mean(table * table, axis=1, keepdims=True) + norm_eps)]
    ppermute x1 -> x0, starting transfers between devices: 1.73 us -> none  [shifted(): return lax.ppermute(block, axis, route)]
    convert_element_type x2 -> x0, other arithmetic: 1.56 us -> none  [the longest x1 1.05 us: local(): returned.astype(jnp.float32)]
    add x2 -> x0, other arithmetic: 1.47 us -> none  [the longest x1 0.78 us: local(): prior = shifted(token_ids[T - 2:] + 1, CTX, 1)]
  transfers between devices with their start and end apart: 1 -> 0, of which waited for: 0 -> 0; matrix products, arithmetic and copies ran while one was open for 4% -> 0% of each run, Pallas kernels for 0% -> 0%
where the time goes in v2:
time: 77.3 us; the launch traced here: 77.2 us
  Pallas kernels  75.1 us (97%)
  local copies, waits for them, and re-layouts  2.06 us (3%)
    pallas_call x1, Pallas kernels, local(): pl.pallas_call(block_kernel, out_shape=jax.ShapeDtypeStruct((T, cols), B)...  75.1 us
    unnamed x1, local copies, waits for them, and re-layouts  2.06 us

profile of v2, /device:TPU:8, one launch (start us, length us, event | category | flops | bytes accessed | tf_op | source)
XLA Modules:
  0.0 77.2 jit_solution(4491921916919159059)
XLA Ops:
  0.0 75.1 %block.1 = bf16[768,512]{1,0:T(8,128)(2,1)} custom-call(s32[6,128]{1,0:T(8,128)} %bitcast.8, f32[1,4096]{1,0:T(1,128)} %bitcast.7, f32[3,3,256]{2,1,0:T(4,128)} %taps_ref.1, f32[2,128]{1,0:T(2,128)} %bitcast.9, f32[192,128]{1,0:T(8,128)} %constant.12.clone.ct_ref, f32[192,128]{1,0:T(8,128)} %constant.13.clone.st_ref, bf16[512,4096]{1,0:T(8,128)(2,1)} %table_hbm.1, ...), custom_call_target="tpu_custom_call" | custom-call | tf_op jit(solution)/shard_map/block/pallas_call | solution.py:335
  75.1 2.1 %copy.16 = bf16[768,512]{1,0:T(8,128)(2,1)} copy(bf16[768,512]{1,0:T(8,128)(2,1)} %block.1) | data formatting | bytes 1572864

commit v3 on v2

v3 whole, which is shorter than its diff:
```python
import functools
import math

import jax
import jax.numpy as jnp
import numpy as np
from jax import lax
from jax.experimental import pallas as pl
from jax.experimental.pallas import tpu as pltpu
from jax.sharding import Mesh
from jax.sharding import PartitionSpec as P

CTX = ("x", "zl", "core")
MESH = pl.DeviceIdType.MESH
PEERS = 32
TP = 8
norm_eps = 1e-06


@functools.lru_cache(maxsize=None)
def tables(peers, per):
    R = peers * per
    N = 256 * R
    order = (np.arange(per)[:, None] + per * np.arange(peers)[None, :]).reshape(-1)
    k1 = np.arange(R) + 0.5
    a1 = 2 * np.pi * np.outer(k1, order) / (2 * R)
    f1 = np.concatenate([np.cos(a1), -np.sin(a1)], 0)
    at = 2 * np.pi * np.outer(k1, np.arange(128)) / N
    a2 = 2 * np.pi * (np.outer(np.arange(128), np.arange(128)) % 128) / 128
    c, s = np.cos(a2), np.sin(a2)
    w2 = np.block([[c, -s], [s, c]])
    w2i = np.block([[c, s], [-s, c]])
    f1i = np.concatenate([np.cos(a1.T), -np.sin(a1.T)], 1)
    return f1, np.cos(at), np.sin(at), w2, w2i, f1i


def peer_of(p):
    return {"x": p // 8, "zl": lax.rem(p // 2, 4), "core": lax.rem(p, 2)}


def ctx_index():
    return lax.axis_index("x") * 8 + lax.axis_index("zl") * 2 + lax.axis_index("core")


def dot(a, b):
    return jnp.dot(a, b, preferred_element_type=jnp.float32)


def send(src, dst, s, r, dev):
    return pltpu.make_async_remote_copy(
        src_ref=src, dst_ref=dst, send_sem=s, recv_sem=r, device_id=dev, device_id_type=MESH
    )


CHUNKS = 6
UNROLL = 3
EARLY = 8


def normalize(tv, gain_ref, nv, first, last):
    width = tv.shape[1]

    @pl.loop(first, last)
    def _(r):
        rows = pl.ds(pl.multiple_of(r * 32, 32), 32)
        acc = jnp.zeros((32, 128), jnp.float32)
        for j in range(width // 128):
            x = tv[rows, j * 128 : (j + 1) * 128].astype(jnp.float32)
            acc += x * x
        scale = lax.rsqrt(jnp.sum(acc, axis=1, keepdims=True) * (1.0 / width) + norm_eps)
        for j in range(width // 128):
            cols = slice(j * 128, (j + 1) * 128)
            x = tv[rows, cols].astype(jnp.float32)
            nv[rows, cols] = (x * scale * gain_ref[:, cols]).astype(jnp.bfloat16)


def upright(row):
    return jnp.transpose(jnp.broadcast_to(row, (128, 128)))


def block_kernel(
    ids_ref, gain_ref, taps_ref, skip_ref, ct_ref, st_ref, table_hbm, w3_hbm, filt_hbm, wo_hbm, f1_hbm, w2_hbm, w2i_hbm, f1i_hbm,
    o_ref,
    tv, nv, wv, hot, wo, f1, w2, w2i, f1i, idall, column, small, rows_t, hx, pf, qf, res, flat, xs, spec, back, bs, sk, ret, buf,
    ld, ids_s, ids_r, fs, fr, xsnd, xrcv, us, ur, ds, dr, ls, lr,
):
    x, zl, core = lax.axis_index("x"), lax.axis_index("zl"), lax.axis_index("core")
    me = ctx_index()
    zh, y = lax.axis_index("zh"), lax.axis_index("y")
    own = zh * 4 + y
    up, down = lax.rem(y + 1, 4), lax.rem(y + 3, 4)
    vocab = tv.shape[0]
    part = small.shape[1]
    T = res.shape[0]
    owned = part // PEERS
    step = T // CHUNKS
    per = T // 128
    R = PEERS * per
    half, inside = me // 16, pl.multiple_of(lax.rem(me, 16) * owned, owned)

    def each_peer(planes, fn):
        def chip(t, skip_self):
            px, pz = lax.rem(x + t // 4, 4), lax.rem(zl + lax.rem(t, 4), 4)
            for dc in range(2):
                pc = lax.rem(core + dc, 2)
                p = px * 8 + pz * 2 + pc
                for k in range(planes):
                    if not (skip_self and dc == 0 and k == 0):
                        dev = {"x": px, "zl": pz, "core": pc}
                        if k == 1:
                            dev["zh"] = 1 - zh
                        fn(p, k, dev)

        def go(t, carry):
            chip(t, False)
            return carry

        lax.fori_loop(1, 16, go, 0, unroll=UNROLL)
        chip(0, True)

    bar = pltpu.get_barrier_semaphore()

    def greet(dev):
        pl.semaphore_signal(bar, inc=1, device_id=dev, device_id_type=MESH)

    each_peer(2, lambda p, k, dev: greet(dev))
    greet({"y": up})
    greet({"y": down})

    loads = [
        pltpu.make_async_copy(a, b, ld.at[i])
        for i, (a, b) in enumerate(
            [(table_hbm, tv)]
            + [(w3_hbm.at[s, :, pl.ds(pl.multiple_of(half * 128, 128), 128)], wv.at[:, pl.ds(s * 128, 128)]) for s in range(3)]
            + [(filt_hbm.at[me], hx.at[me]), (f1_hbm, f1), (w2_hbm, w2), (w2i_hbm, w2i), (f1i_hbm, f1i), (wo_hbm, wo)]
        )
    ]
    for c in loads:
        c.start()

    for r in range(3):
        for s in range(3):
            row = jnp.where(half == 0, taps_ref[r, s : s + 1, 0:128], taps_ref[r, s : s + 1, 128:256])
            column[...] = upright(row)
            rows_t[r * 3 + s] = column[pl.ds(inside, owned), :]
    column[...] = upright(jnp.where(half == 0, skip_ref[0:1, :], skip_ref[1:2, :]))
    rows_t[9] = column[pl.ds(inside, owned), :]
    idall[me] = ids_ref[...]
    loads[0].wait()
    normalize(tv, gain_ref, nv, 0, EARLY)

    pl.semaphore_wait(bar, 2 * PEERS + 1)

    each_peer(1, lambda p, k, dev: send(ids_ref, idall.at[me], ids_s, ids_r, dev).start())
    each_peer(1, lambda p, k, dev: send(filt_hbm.at[p], hx.at[me], fs, fr, dev).start())

    def all_of(ref, s, r):
        most = ref.at[pl.ds(0, PEERS - 1)]
        return send(most, most, s, r, {"y": up})

    normalize(tv, gain_ref, nv, EARLY, vocab // 32)
    for s in range(3):
        loads[1 + s].wait()
    table_rows = []
    for n0, n1 in ((0, 256), (256, 384)):
        projected = dot(nv[...], wv[:, n0:n1]).astype(jnp.bfloat16).astype(jnp.float32)
        for n in range(n0, n1, 128):
            for v in range(vocab // 128):
                flat[v * 128 : (v + 1) * 128, :] = jnp.transpose(projected[v * 128 : (v + 1) * 128, n - n0 : n - n0 + 128])
            table_rows.append(
                jnp.concatenate([flat[pl.ds(pl.multiple_of(v * 128 + inside, owned), owned), :] for v in range(vocab // 128)], axis=1)
            )
    picks = jnp.concatenate(table_rows, axis=0).astype(jnp.bfloat16)

    all_of(idall, ids_s, ids_r).wait_recv()
    lane = lax.broadcasted_iota(jnp.int32, (owned, 128), 1)
    token = lax.broadcasted_iota(jnp.int32, (vocab, 128), 0)

    def positions(i, carry):
        for q2 in range(per // 2):
            hits = [
                (jnp.broadcast_to(idall[i, q : q + 1, :], (vocab, 128)) == token).astype(jnp.float32).astype(jnp.bfloat16)
                for q in (2 * q2, 2 * q2 + 1)
            ]
            chosen = dot(picks, jnp.concatenate(hits, axis=1))
            for h in range(2):
                q = 2 * q2 + h
                short, later = [], []
                for s in range(3):
                    now = chosen[s * owned : (s + 1) * owned, h * 128 : (h + 1) * 128]
                    by1, by2 = pltpu.roll(now, 1, 1), pltpu.roll(now, 2, 1)
                    before1, before2 = carry[s]
                    one = jnp.where(lane < 1, before1, by1)
                    two = jnp.where(lane < 2, before2, by2)
                    short.append(
                        (rows_t[s] * now + rows_t[3 + s] * one + rows_t[6 + s] * two).astype(jnp.bfloat16).astype(jnp.float32)
                    )
                    later.append((by1, by2))
                carry = tuple(later)
                rows = pl.ds(pl.multiple_of(q * part + i * owned, owned), owned)
                pf[rows, :] = (short[1] * short[2]).astype(jnp.bfloat16).astype(jnp.float32)
                qf[rows, :] = short[0]
        return carry

    nothing = jnp.zeros((owned, 128), jnp.float32)
    lax.fori_loop(0, PEERS, positions, ((nothing, nothing),) * 3, unroll=4)

    def forward(src, slot):
        for c in range(owned):
            for q in range(per):
                xs[q * PEERS : (q + 1) * PEERS, c * 128 : (c + 1) * 128] = src[
                    pl.ds(q * part + c, PEERS, stride=owned), :
                ].astype(jnp.bfloat16)
        ct, st = ct_ref[...], st_ref[...]
        for c2 in range(owned // 2):
            first = dot(f1[...], xs[:, c2 * 256 : (c2 + 1) * 256])
            for h in range(2):
                c = 2 * c2 + h
                re = first[:R, h * 128 : h * 128 + 128]
                im = first[R:, h * 128 : h * 128 + 128]
                rows = slice(c * R, (c + 1) * R)
                back[rows, 0:128] = (re * ct + im * st).astype(jnp.bfloat16)
                back[rows, 128:256] = (im * ct - re * st).astype(jnp.bfloat16)
        for c in range(owned):
            rows = slice(c * R, (c + 1) * R)
            spec[slot, rows, :] = dot(back[rows, :], w2[...])

    for i in range(4, 9):
        loads[i].wait()
    forward(pf, 0)
    all_of(hx, fs, fr).wait_recv()
    for q in range(per):
        flat[q * part : (q + 1) * part, :] = hx[:, :, q * 128 : (q + 1) * 128].astype(jnp.float32).reshape(part, 128)
    forward(flat, 1)
    ct, st = ct_ref[...], st_ref[...]
    for c in range(owned):
        rows = slice(c * R, (c + 1) * R)
        ar, ai = spec[0, rows, 0:128], spec[0, rows, 128:256]
        br, bi = spec[1, rows, 0:128], spec[1, rows, 128:256]
        back[rows, 0:128] = (ar * br - ai * bi).astype(jnp.bfloat16)
        back[rows, 128:256] = (ar * bi + ai * br).astype(jnp.bfloat16)
        u = dot(back[rows, :], w2i[...])
        ur_, ui_ = u[:, 0:128], u[:, 128:256]
        bs[0:R, c * 128 : (c + 1) * 128] = (ur_ * ct - ui_ * st).astype(jnp.bfloat16)
        bs[R : 2 * R, c * 128 : (c + 1) * 128] = (ui_ * ct + ur_ * st).astype(jnp.bfloat16)
    scale = 2.0 / (256 * R)
    for c2 in range(owned // 2):
        z = dot(f1i[...], bs[:, c2 * 256 : (c2 + 1) * 256]) * scale
        for h in range(2):
            c = 2 * c2 + h
            for q in range(per):
                flat[pl.ds(q * part + c, PEERS, stride=owned), :] = z[q * PEERS : (q + 1) * PEERS, h * 128 : h * 128 + 128]

    def cols_of(q):
        return pl.ds(q * step, step)

    for q in range(CHUNKS):
        rows = slice(q * part, (q + 1) * part)
        gain = jnp.broadcast_to(rows_t[9][None], (PEERS, owned, 128)).reshape(part, 128)
        skipped = (flat[rows, :] + gain * pf[rows, :]).astype(jnp.bfloat16).astype(jnp.float32)
        gated = (qf[rows, :] * skipped).astype(jnp.bfloat16)
        sk[:, :, q * step : (q + 1) * step] = gated.reshape(PEERS, owned, 128)
        each_peer(
            2, lambda p, k, dev: send(sk.at[p, :, cols_of(q)], ret.at[k, me, :, cols_of(q)], xsnd.at[k, q], xrcv.at[k, q], dev).start()
        )
        ret[0, me, :, q * step : (q + 1) * step] = sk[me, :, q * step : (q + 1) * step]

    lanes = lax.broadcasted_iota(jnp.int32, (128, 128), 1)
    for b in range(per):
        col = upright(ids_ref[b : b + 1, :])
        for j in range(vocab // 128):
            hot[b * 128 : (b + 1) * 128, j * 128 : (j + 1) * 128] = (col == lanes + 128 * j).astype(jnp.float32).astype(jnp.bfloat16)
    width = o_ref.shape[1]
    res[...] = dot(hot[...], tv[:, pl.ds(pl.multiple_of(own * width, width), width)]).astype(jnp.bfloat16)
    loads[9].wait()

    def slot_of(k, yy):
        return (zh if k == 0 else 1 - zh) * 4 + yy

    def direct(k, c, upward):
        here = buf.at[slot_of(k, y), cols_of(c)]
        s, r = (us, ur) if upward else (ds, dr)
        return send(here, here, s.at[k, c], r.at[k, c], {"y": up if upward else down})

    def relay(k, c):
        upward = (c + k) % 2 == 0
        here = buf.at[slot_of(k, down if upward else up), cols_of(c)]
        return send(here, here, ls.at[k, c], lr.at[k, c], {"y": up if upward else down})

    def returned(k, q):
        most = ret.at[k, pl.ds(0, PEERS - 1 + k), :, cols_of(q)]
        return send(most, most, xsnd.at[k, q], xrcv.at[k, q], {"y": up})

    def turn(k, q):
        returned(k, q).wait_recv()
        rows = slice(q * step, (q + 1) * step)
        arrived = ret[k, :, :, rows].astype(jnp.float32).reshape(part, step)
        buf[slot_of(k, y), rows, :] = jnp.transpose(arrived).astype(jnp.bfloat16)
        direct(k, q, True).start()
        direct(k, q, False).start()

    def pass_on(k, c):
        direct(k, c, (c + k) % 2 == 0).wait_recv()
        relay(k, c).start()

    def finish(c):
        rows = slice(c * step, (c + 1) * step)
        for k in range(2):
            direct(k, c, (c + k) % 2 == 1).wait_recv()
            relay(k, c).wait_recv()
        acc = res[rows, :].astype(jnp.float32)
        for j in range(TP):
            acc += dot(buf[j, rows, :], wo[j * part : (j + 1) * part, :])
        o_ref[rows, :] = acc.astype(jnp.bfloat16)

    for s in range(CHUNKS + 3):
        for k in range(2):
            if s < CHUNKS:
                turn(k, s)
            if 0 <= s - 1 < CHUNKS:
                pass_on(k, s - 1)
        if 0 <= s - 3 < CHUNKS:
            finish(s - 3)

    all_of(idall, ids_s, ids_r).wait_send()
    all_of(hx, fs, fr).wait_send()
    for c in range(CHUNKS):
        for k in range(2):
            returned(k, c).wait_send()
            direct(k, c, True).wait_send()
            direct(k, c, False).wait_send()
            relay(k, c).wait_send()


def local(token_ids, embed_table, norm_gain, w_in, short_taps, long_filter, skip_gain, w_out):
    vocab, width = embed_table.shape
    T = token_ids.shape[0]
    part = w_in.shape[2]
    owned = part // PEERS
    per = T // 128
    R = PEERS * per
    cols = w_out.shape[1]
    f1, ct, st, w2, w2i, f1i = tables(PEERS, per)
    bf = lambda a: jnp.asarray(a.astype(jnp.bfloat16))
    f32 = lambda a: jnp.asarray(a.astype(np.float32))
    vmem = pl.BlockSpec(memory_space=pltpu.VMEM)
    hbm = pl.BlockSpec(memory_space=pl.ANY)
    dma = pltpu.SemaphoreType.DMA
    B, F = jnp.bfloat16, jnp.float32
    V = pltpu.VMEM
    return pl.pallas_call(
        block_kernel,
        out_shape=jax.ShapeDtypeStruct((T, cols), B),
        in_specs=[vmem] * 6 + [hbm] * 8,
        out_specs=vmem,
        scratch_shapes=[
            V((vocab, width), B),
            V((vocab, width), B),
            V((width, 384), B),
            V((T, vocab), B),
            V(w_out.shape, B),
            V(f1.shape, B),
            V(w2.shape, B),
            V(w2i.shape, B),
            V(f1i.shape, B),
            V((PEERS, per, 128), jnp.int32),
            V((128, 128), F),
            V((8, part), F),
            V((10, owned, 128), F),
            V((PEERS, owned, T), B),
            V((per * part, 128), F),
            V((per * part, 128), F),
            V((T, cols), B),
            V((per * part, 128), F),
            V((R, owned * 128), B),
            V((2, owned * R, 256), F),
            V((owned * R, 256), B),
            V((2 * R, owned * 128), B),
            V((PEERS, owned, T), B),
            V((2, PEERS, owned, T), B),
            V((TP, T, part), B),
            dma((10,)),
            dma,
            dma,
            dma,
            dma,
        ]
        + [dma((2, CHUNKS))] * 8,
        compiler_params=pltpu.CompilerParams(collective_id=0, has_side_effects=True, vmem_limit_bytes=60 * 2**20),
        name="block",
    )(
        token_ids.reshape(per, 128),
        norm_gain.reshape(1, width),
        short_taps,
        skip_gain.reshape(part // 128, 128),
        f32(ct),
        f32(st),
        embed_table,
        jnp.transpose(w_in, (1, 0, 2)),
        long_filter.reshape(PEERS, owned, T),
        w_out,
        bf(f1),
        bf(w2),
        bf(w2i),
        bf(f1i),
    )


def solution(mesh):
    finer = Mesh(mesh.devices.reshape(4, 4, 2, 2, 4), ("x", "zl", "core", "zh", "y"))
    tp = ("zh", "y")
    in_specs = (
        P(CTX),
        P(),
        P(),
        P(None, None, tp),
        P(None, None, tp),
        P(tp, CTX),
        P(tp),
        P(None, tp),
    )
    return jax.shard_map(local, mesh=finer, in_specs=in_specs, out_specs=P(CTX, tp), check_vma=False)
```

time: 77.3 us -> 68 us (0.88)
  Pallas kernels: 75.1 us -> 65.8 us
    pallas_call x1, Pallas kernels: 75.1 us -> 65.8 us  [local(): pl.pallas_call(block_kernel, out_shape=jax.ShapeDtypeStruct((T, cols), B)...]
where the time goes in v3:
time: 68 us; the launch traced here: 67.8 us
  Pallas kernels  65.8 us (97%)
  local copies, waits for them, and re-layouts  2.06 us (3%)
    pallas_call x1, Pallas kernels, local(): pl.pallas_call(block_kernel, out_shape=jax.ShapeDtypeStruct((T, cols), B)...  65.8 us
    unnamed x1, local copies, waits for them, and re-layouts  2.06 us

profile of v3, /device:TPU:8, one launch (start us, length us, event | category | flops | bytes accessed | tf_op | source)
XLA Modules:
  0.0 67.8 jit_solution(16554890323999955222)
XLA Ops:
  0.0 65.8 %block.1 = bf16[768,512]{1,0:T(8,128)(2,1)} custom-call(s32[6,128]{1,0:T(8,128)} %bitcast.8, f32[1,4096]{1,0:T(1,128)} %bitcast.7, f32[3,3,256]{2,1,0:T(4,128)} %taps_ref.1, f32[2,128]{1,0:T(2,128)} %bitcast.9, f32[192,128]{1,0:T(8,128)} %constant.12.clone.ct_ref, f32[192,128]{1,0:T(8,128)} %constant.13.clone.st_ref, bf16[512,4096]{1,0:T(8,128)(2,1)} %table_hbm.1, ...), custom_call_target="tpu_custom_call" | custom-call | tf_op jit(solution)/shard_map/block/pallas_call | solution.py:351
  65.8 2.1 %copy.16 = bf16[768,512]{1,0:T(8,128)(2,1)} copy(bf16[768,512]{1,0:T(8,128)(2,1)} %block.1) | data formatting | bytes 1572864

commit v4 on v3

--- a/solution.py
+++ b/solution.py
@@ -79,9 +79,9 @@
 
 
 def block_kernel(
-    ids_ref, gain_ref, taps_ref, skip_ref, ct_ref, st_ref, table_hbm, w3_hbm, filt_hbm, wo_hbm, f1_hbm, w2_hbm, w2i_hbm, f1i_hbm,
+    ids_hbm, gain_hbm, taps_hbm, skip_hbm, ct_hbm, st_hbm, table_hbm, w3_hbm, filt_hbm, wo_hbm, f1_hbm, w2_hbm, w2i_hbm, f1i_hbm,
     o_ref,
-    tv, nv, wv, hot, wo, f1, w2, w2i, f1i, idall, column, small, rows_t, hx, pf, qf, res, flat, xs, spec, back, bs, sk, ret, buf,
+    ids_ref, gain_ref, taps_ref, skip_ref, ct_ref, st_ref, fv, tv, nv, wv, hot, wo, f1, w2, w2i, f1i, idall, column, small, rows_t, hx, pf, qf, res, flat, xs, spec, back, bs, sk, ret, buf,
     ld, ids_s, ids_r, fs, fr, xsnd, xrcv, us, ur, ds, dr, ls, lr,
 ):
     x, zl, core = lax.axis_index("x"), lax.axis_index("zl"), lax.axis_index("core")
@@ -130,13 +130,33 @@
     loads = [
         pltpu.make_async_copy(a, b, ld.at[i])
         for i, (a, b) in enumerate(
-            [(table_hbm, tv)]
+            [(table_hbm, tv), (gain_hbm, gain_ref), (ids_hbm, ids_ref), (filt_hbm, fv), (taps_hbm, taps_ref), (skip_hbm, skip_ref)]
             + [(w3_hbm.at[s, :, pl.ds(pl.multiple_of(half * 128, 128), 128)], wv.at[:, pl.ds(s * 128, 128)]) for s in range(3)]
-            + [(filt_hbm.at[me], hx.at[me]), (f1_hbm, f1), (w2_hbm, w2), (w2i_hbm, w2i), (f1i_hbm, f1i), (wo_hbm, wo)]
+            + [(ct_hbm, ct_ref), (st_hbm, st_ref), (f1_hbm, f1), (w2_hbm, w2), (w2i_hbm, w2i), (f1i_hbm, f1i), (wo_hbm, wo)]
         )
     ]
     for c in loads:
         c.start()
+
+    for i in range(2):
+        loads[i].wait()
+    normalize(tv, gain_ref, nv, 0, EARLY)
+    for i in range(2, 4):
+        loads[i].wait()
+
+    pl.semaphore_wait(bar, 2 * PEERS + 1)
+
+    each_peer(1, lambda p, k, dev: send(ids_ref, idall.at[me], ids_s, ids_r, dev).start())
+    each_peer(1, lambda p, k, dev: send(fv.at[p], hx.at[me], fs, fr, dev).start())
+
+    def all_of(ref, s, r):
+        most = ref.at[pl.ds(0, PEERS - 1)]
+        return send(most, most, s, r, {"y": up})
+
+    idall[me] = ids_ref[...]
+    hx[me] = fv[me]
+    for i in range(4, 6):
+        loads[i].wait()
 
     for r in range(3):
         for s in range(3):
@@ -145,49 +165,39 @@
             rows_t[r * 3 + s] = column[pl.ds(inside, owned), :]
     column[...] = upright(jnp.where(half == 0, skip_ref[0:1, :], skip_ref[1:2, :]))
     rows_t[9] = column[pl.ds(inside, owned), :]
-    idall[me] = ids_ref[...]
-    loads[0].wait()
-    normalize(tv, gain_ref, nv, 0, EARLY)
-
-    pl.semaphore_wait(bar, 2 * PEERS + 1)
-
-    each_peer(1, lambda p, k, dev: send(ids_ref, idall.at[me], ids_s, ids_r, dev).start())
-    each_peer(1, lambda p, k, dev: send(filt_hbm.at[p], hx.at[me], fs, fr, dev).start())
-
-    def all_of(ref, s, r):
-        most = ref.at[pl.ds(0, PEERS - 1)]
-        return send(most, most, s, r, {"y": up})
-
     normalize(tv, gain_ref, nv, EARLY, vocab // 32)
     for s in range(3):
-        loads[1 + s].wait()
+        loads[6 + s].wait()
     table_rows = []
     for n0, n1 in ((0, 256), (256, 384)):
         projected = dot(nv[...], wv[:, n0:n1]).astype(jnp.bfloat16).astype(jnp.float32)
         for n in range(n0, n1, 128):
             for v in range(vocab // 128):
                 flat[v * 128 : (v + 1) * 128, :] = jnp.transpose(projected[v * 128 : (v + 1) * 128, n - n0 : n - n0 + 128])
-            table_rows.append(
-                jnp.concatenate([flat[pl.ds(pl.multiple_of(v * 128 + inside, owned), owned), :] for v in range(vocab // 128)], axis=1)
-            )
-    picks = jnp.concatenate(table_rows, axis=0).astype(jnp.bfloat16)
+            table_rows.append([flat[pl.ds(pl.multiple_of(v * 128 + inside, owned), owned), :] for v in range(vocab // 128)])
+    groups = vocab // 128
+    picks = jnp.concatenate([table_rows[s][v] for v in range(groups) for s in range(3)], axis=0).astype(jnp.bfloat16)
 
     all_of(idall, ids_s, ids_r).wait_recv()
     lane = lax.broadcasted_iota(jnp.int32, (owned, 128), 1)
-    token = lax.broadcasted_iota(jnp.int32, (vocab, 128), 0)
+    token = lax.broadcasted_iota(jnp.int32, (128, 128), 0)
 
     def positions(i, carry):
         for q2 in range(per // 2):
-            hits = [
-                (jnp.broadcast_to(idall[i, q : q + 1, :], (vocab, 128)) == token).astype(jnp.float32).astype(jnp.bfloat16)
-                for q in (2 * q2, 2 * q2 + 1)
-            ]
+            pair = [idall[i, q : q + 1, :] for q in (2 * q2, 2 * q2 + 1)]
+            hits = [(jnp.broadcast_to(ids & 127, (128, 128)) == token).astype(jnp.float32).astype(jnp.bfloat16) for ids in pair]
             chosen = dot(picks, jnp.concatenate(hits, axis=1))
             for h in range(2):
                 q = 2 * q2 + h
+                group = jnp.broadcast_to(pair[h] >> 7, (owned, 128))
                 short, later = [], []
                 for s in range(3):
-                    now = chosen[s * owned : (s + 1) * owned, h * 128 : (h + 1) * 128]
+                    of = [
+                        chosen[(v * 3 + s) * owned : (v * 3 + s + 1) * owned, h * 128 : (h + 1) * 128] for v in range(groups)
+                    ]
+                    now = of[0]
+                    for v in range(1, groups):
+                        now = jnp.where(group == v, of[v], now)
                     by1, by2 = pltpu.roll(now, 1, 1), pltpu.roll(now, 2, 1)
                     before1, before2 = carry[s]
                     one = jnp.where(lane < 1, before1, by1)
@@ -225,7 +235,7 @@
             rows = slice(c * R, (c + 1) * R)
             spec[slot, rows, :] = dot(back[rows, :], w2[...])
 
-    for i in range(4, 9):
+    for i in range(9, 15):
         loads[i].wait()
     forward(pf, 0)
     all_of(hx, fs, fr).wait_recv()
@@ -272,7 +282,7 @@
             hot[b * 128 : (b + 1) * 128, j * 128 : (j + 1) * 128] = (col == lanes + 128 * j).astype(jnp.float32).astype(jnp.bfloat16)
     width = o_ref.shape[1]
     res[...] = dot(hot[...], tv[:, pl.ds(pl.multiple_of(own * width, width), width)]).astype(jnp.bfloat16)
-    loads[9].wait()
+    loads[15].wait()
 
     def slot_of(k, yy):
         return (zh if k == 0 else 1 - zh) * 4 + yy
@@ -351,9 +361,16 @@
     return pl.pallas_call(
         block_kernel,
         out_shape=jax.ShapeDtypeStruct((T, cols), B),
-        in_specs=[vmem] * 6 + [hbm] * 8,
+        in_specs=[hbm] * 14,
         out_specs=vmem,
         scratch_shapes=[
+            V((per, 128), jnp.int32),
+            V((1, width), F),
+            V(short_taps.shape, F),
+            V((part // 128, 128), F),
+            V(ct.shape, F),
+            V(st.shape, F),
+            V((PEERS, owned, T), B),
             V((vocab, width), B),
             V((vocab, width), B),
             V((width, 384), B),
@@ -379,7 +396,7 @@
             V((PEERS, owned, T), B),
             V((2, PEERS, owned, T), B),
             V((TP, T, part), B),
-            dma((10,)),
+            dma((16,)),
             dma,
             dma,
             dma,

time: 68 us -> 66.2 us (0.974)
  Pallas kernels: 65.8 us -> 64 us
    pallas_call x1, Pallas kernels: 65.8 us -> 64 us  [local(): pl.pallas_call(block_kernel, out_shape=jax.ShapeDtypeStruct((T, cols), B)...]
where the time goes in v4:
time: 66.2 us; the launch traced here: 66.1 us
  Pallas kernels  64 us (97%)
  local copies, waits for them, and re-layouts  2.06 us (3%)
    pallas_call x1, Pallas kernels, local(): pl.pallas_call(block_kernel, out_shape=jax.ShapeDtypeStruct((T, cols), B)...  64 us
    unnamed x1, local copies, waits for them, and re-layouts  2.06 us

profile of v4, /device:TPU:8, one launch (start us, length us, event | category | flops | bytes accessed | tf_op | source)
XLA Modules:
  0.0 66.1 jit_solution(7216265329951706421)
XLA Ops:
  0.0 64.0 %block.1 = bf16[768,512]{1,0:T(8,128)(2,1)} custom-call(s32[6,128]{1,0:T(8,128)} %bitcast.8, f32[1,4096]{1,0:T(1,128)} %bitcast.7, f32[3,3,256]{2,1,0:T(4,128)} %taps_hbm.1, f32[2,128]{1,0:T(2,128)} %bitcast.9, f32[192,128]{1,0:T(8,128)} %constant.12.clone.ct_hbm, f32[192,128]{1,0:T(8,128)} %constant.13.clone.st_hbm, bf16[512,4096]{1,0:T(8,128)(2,1)} %table_hbm.1, ...), custom_call_target="tpu_custom_call" | custom-call | tf_op jit(solution)/shard_map/block/pallas_call | solution.py:361
  64.0 2.1 %copy.16 = bf16[768,512]{1,0:T(8,128)(2,1)} copy(bf16[768,512]{1,0:T(8,128)(2,1)} %block.1) | data formatting | bytes 1572864

commit v5 on v4

--- a/solution.py
+++ b/solution.py
@@ -54,7 +54,6 @@
 
 CHUNKS = 6
 UNROLL = 3
-EARLY = 8
 
 
 def normalize(tv, gain_ref, nv, first, last):
@@ -81,7 +80,7 @@
 def block_kernel(
     ids_hbm, gain_hbm, taps_hbm, skip_hbm, ct_hbm, st_hbm, table_hbm, w3_hbm, filt_hbm, wo_hbm, f1_hbm, w2_hbm, w2i_hbm, f1i_hbm,
     o_ref,
-    ids_ref, gain_ref, taps_ref, skip_ref, ct_ref, st_ref, fv, tv, nv, wv, hot, wo, f1, w2, w2i, f1i, idall, column, small, rows_t, hx, pf, qf, res, flat, xs, spec, back, bs, sk, ret, buf,
+    ids_ref, gain_ref, taps_ref, skip_ref, ct_ref, st_ref, fv, tv, nv, wv, hot, wo, f1, w2, w2i, f1i, idpair, idall, column, small, rows_t, hx, pf, qf, res, flat, xs, spec, back, bs, sk, ret, buf,
     ld, ids_s, ids_r, fs, fr, xsnd, xrcv, us, ur, ds, dr, ls, lr,
 ):
     x, zl, core = lax.axis_index("x"), lax.axis_index("zl"), lax.axis_index("core")
@@ -99,12 +98,14 @@
     half, inside = me // 16, pl.multiple_of(lax.rem(me, 16) * owned, owned)
 
     def each_peer(planes, fn):
+        planes = range(planes) if isinstance(planes, int) else planes
+
         def chip(t, skip_self):
             px, pz = lax.rem(x + t // 4, 4), lax.rem(zl + lax.rem(t, 4), 4)
             for dc in range(2):
                 pc = lax.rem(core + dc, 2)
                 p = px * 8 + pz * 2 + pc
-                for k in range(planes):
+                for k in planes:
                     if not (skip_self and dc == 0 and k == 0):
                         dev = {"x": px, "zl": pz, "core": pc}
                         if k == 1:
@@ -130,7 +131,7 @@
     loads = [
         pltpu.make_async_copy(a, b, ld.at[i])
         for i, (a, b) in enumerate(
-            [(table_hbm, tv), (gain_hbm, gain_ref), (ids_hbm, ids_ref), (filt_hbm, fv), (taps_hbm, taps_ref), (skip_hbm, skip_ref)]
+            [(ids_hbm, ids_ref), (filt_hbm, fv), (table_hbm, tv), (gain_hbm, gain_ref), (taps_hbm, taps_ref), (skip_hbm, skip_ref)]
             + [(w3_hbm.at[s, :, pl.ds(pl.multiple_of(half * 128, 128), 128)], wv.at[:, pl.ds(s * 128, 128)]) for s in range(3)]
             + [(ct_hbm, ct_ref), (st_hbm, st_ref), (f1_hbm, f1), (w2_hbm, w2), (w2i_hbm, w2i), (f1i_hbm, f1i), (wo_hbm, wo)]
         )
@@ -140,20 +141,17 @@
 
     for i in range(2):
         loads[i].wait()
-    normalize(tv, gain_ref, nv, 0, EARLY)
-    for i in range(2, 4):
-        loads[i].wait()
-
+    idpair[...] = ids_ref[0 : per // 2, :] + ids_ref[per // 2 : per, :] * 65536
     pl.semaphore_wait(bar, 2 * PEERS + 1)
 
-    each_peer(1, lambda p, k, dev: send(ids_ref, idall.at[me], ids_s, ids_r, dev).start())
+    each_peer(1, lambda p, k, dev: send(idpair, idall.at[me], ids_s, ids_r, dev).start())
     each_peer(1, lambda p, k, dev: send(fv.at[p], hx.at[me], fs, fr, dev).start())
 
     def all_of(ref, s, r):
         most = ref.at[pl.ds(0, PEERS - 1)]
         return send(most, most, s, r, {"y": up})
 
-    idall[me] = ids_ref[...]
+    idall[me] = idpair[...]
     hx[me] = fv[me]
     for i in range(4, 6):
         loads[i].wait()
@@ -165,7 +163,9 @@
             rows_t[r * 3 + s] = column[pl.ds(inside, owned), :]
     column[...] = upright(jnp.where(half == 0, skip_ref[0:1, :], skip_ref[1:2, :]))
     rows_t[9] = column[pl.ds(inside, owned), :]
-    normalize(tv, gain_ref, nv, EARLY, vocab // 32)
+    for i in range(2, 4):
+        loads[i].wait()
+    normalize(tv, gain_ref, nv, 0, vocab // 32)
     for s in range(3):
         loads[6 + s].wait()
     table_rows = []
@@ -184,7 +184,8 @@
 
     def positions(i, carry):
         for q2 in range(per // 2):
-            pair = [idall[i, q : q + 1, :] for q in (2 * q2, 2 * q2 + 1)]
+            pair = [idall[i, q % (per // 2) : q % (per // 2) + 1, :] for q in (2 * q2, 2 * q2 + 1)]
+            pair = [ids & 65535 if 2 * q2 + h < per // 2 else ids >> 16 for h, ids in enumerate(pair)]
             hits = [(jnp.broadcast_to(ids & 127, (128, 128)) == token).astype(jnp.float32).astype(jnp.bfloat16) for ids in pair]
             chosen = dot(picks, jnp.concatenate(hits, axis=1))
             for h in range(2):
@@ -270,9 +271,11 @@
         skipped = (flat[rows, :] + gain * pf[rows, :]).astype(jnp.bfloat16).astype(jnp.float32)
         gated = (qf[rows, :] * skipped).astype(jnp.bfloat16)
         sk[:, :, q * step : (q + 1) * step] = gated.reshape(PEERS, owned, 128)
-        each_peer(
-            2, lambda p, k, dev: send(sk.at[p, :, cols_of(q)], ret.at[k, me, :, cols_of(q)], xsnd.at[k, q], xrcv.at[k, q], dev).start()
-        )
+        for plane in range(2):
+            each_peer(
+                (plane,),
+                lambda p, k, dev: send(sk.at[p, :, cols_of(q)], ret.at[k, me, :, cols_of(q)], xsnd.at[k, q], xrcv.at[k, q], dev).start(),
+            )
         ret[0, me, :, q * step : (q + 1) * step] = sk[me, :, q * step : (q + 1) * step]
 
     lanes = lax.broadcasted_iota(jnp.int32, (128, 128), 1)
@@ -354,10 +357,26 @@
     bf = lambda a: jnp.asarray(a.astype(jnp.bfloat16))
     f32 = lambda a: jnp.asarray(a.astype(np.float32))
     vmem = pl.BlockSpec(memory_space=pltpu.VMEM)
-    hbm = pl.BlockSpec(memory_space=pl.ANY)
+    hbm = pl.BlockSpec(memory_space=pltpu.HBM)
     dma = pltpu.SemaphoreType.DMA
     B, F = jnp.bfloat16, jnp.float32
     V = pltpu.VMEM
+    operands = (
+        token_ids.reshape(per, 128),
+        norm_gain.reshape(1, width),
+        short_taps,
+        skip_gain.reshape(part // 128, 128),
+        f32(ct),
+        f32(st),
+        embed_table,
+        jnp.transpose(w_in, (1, 0, 2)),
+        long_filter.reshape(PEERS, owned, T),
+        w_out,
+        bf(f1),
+        bf(w2),
+        bf(w2i),
+        bf(f1i),
+    )
     return pl.pallas_call(
         block_kernel,
         out_shape=jax.ShapeDtypeStruct((T, cols), B),
@@ -380,7 +399,8 @@
             V(w2.shape, B),
             V(w2i.shape, B),
             V(f1i.shape, B),
-            V((PEERS, per, 128), jnp.int32),
+            V((per // 2, 128), jnp.int32),
+            V((PEERS, per // 2, 128), jnp.int32),
             V((128, 128), F),
             V((8, part), F),
             V((10, owned, 128), F),
@@ -403,24 +423,9 @@
             dma,
         ]
         + [dma((2, CHUNKS))] * 8,
-        compiler_params=pltpu.CompilerParams(collective_id=0, has_side_effects=True, vmem_limit_bytes=60 * 2**20),
+        compiler_params=pltpu.CompilerParams(collective_id=0, has_side_effects=True, vmem_limit_bytes=48 * 2**20),
         name="block",
-    )(
-        token_ids.reshape(per, 128),
-        norm_gain.reshape(1, width),
-        short_taps,
-        skip_gain.reshape(part // 128, 128),
-        f32(ct),
-        f32(st),
-        embed_table,
-        jnp.transpose(w_in, (1, 0, 2)),
-        long_filter.reshape(PEERS, owned, T),
-        w_out,
-        bf(f1),
-        bf(w2),
-        bf(w2i),
-        bf(f1i),
-    )
+    )(*(pltpu.with_memory_space_constraint(a, pltpu.HBM) for a in operands))
 
 
 def solution(mesh):

time: 66.2 us -> 62.8 us (0.949)
  Pallas kernels: 64 us -> 61.6 us
  local copies, waits for them, and re-layouts: 2.06 us -> 0.88 us
    pallas_call x1, Pallas kernels: 64 us -> 61.6 us  [local(): pl.pallas_call(block_kernel, out_shape=jax.ShapeDtypeStruct((T, cols), B)...]
    unnamed x1, local copies, waits for them, and re-layouts: 2.06 us -> 0.88 us
where the time goes in v5:
time: 62.8 us; the launch traced here: 62.5 us
  Pallas kernels  61.6 us (98%)
  local copies, waits for them, and re-layouts  0.88 us (1%)
    pallas_call x1, Pallas kernels, local(): pl.pallas_call(block_kernel, out_shape=jax.ShapeDtypeStruct((T, cols), B)...  61.6 us

profile of v5, /device:TPU:8, one launch (start us, length us, event | category | flops | bytes accessed | tf_op | source)
XLA Modules:
  0.0 62.5 jit_solution(1076869993240979388)
XLA Ops:
  0.0 61.6 %block.1 = bf16[768,512]{1,0:T(8,128)(2,1)S(1)} custom-call(s32[6,128]{1,0:T(8,128)} %bitcast.8, f32[1,4096]{1,0:T(1,128)} %bitcast.7, f32[3,3,256]{2,1,0:T(4,128)} %taps_hbm.1, f32[2,128]{1,0:T(2,128)} %bitcast.9, f32[192,128]{1,0:T(8,128)} %constant.12.clone.ct_hbm, f32[192,128]{1,0:T(8,128)} %constant.13.clone.st_hbm, bf16[512,4096]{1,0:T(8,128)(2,1)} %table_hbm.1, ...), custom_call_target="tpu_custom_call" | custom-call | tf_op jit(solution)/shard_map/block/pallas_call | solution.py:380
  61.6 0.9 %copy.16 = bf16[768,512]{1,0:T(8,128)(2,1)} copy(bf16[768,512]{1,0:T(8,128)(2,1)S(1)} %block.1) | data formatting | bytes 1572864

commit v6 on v5

--- a/solution.py
+++ b/solution.py
@@ -52,7 +52,7 @@
     )
 
 
-CHUNKS = 6
+SPANS = 3
 UNROLL = 3
 
 
@@ -80,60 +80,80 @@
 def block_kernel(
     ids_hbm, gain_hbm, taps_hbm, skip_hbm, ct_hbm, st_hbm, table_hbm, w3_hbm, filt_hbm, wo_hbm, f1_hbm, w2_hbm, w2i_hbm, f1i_hbm,
     o_ref,
-    ids_ref, gain_ref, taps_ref, skip_ref, ct_ref, st_ref, fv, tv, nv, wv, hot, wo, f1, w2, w2i, f1i, idpair, idall, column, small, rows_t, hx, pf, qf, res, flat, xs, spec, back, bs, sk, ret, buf,
-    ld, ids_s, ids_r, fs, fr, xsnd, xrcv, us, ur, ds, dr, ls, lr,
+    ids_ref, gain_ref, taps_ref, skip_ref, ct_ref, st_ref, fv, tv, nv, wv, rt, halves, picks, hot, wo, f1, w2, w2i, f1i, idpair, idall, column, rows_t, hx, pf, qf, res, flat, xs, spec, back, bs, sk, ret, buf,
+    ld, ids_s, ids_r, fs, fr, pk_s, pk_r, xsnd, xrcv, us, ur, ds, dr, ls, lr,
 ):
     x, zl, core = lax.axis_index("x"), lax.axis_index("zl"), lax.axis_index("core")
     me = ctx_index()
     zh, y = lax.axis_index("zh"), lax.axis_index("y")
     own = zh * 4 + y
     up, down = lax.rem(y + 1, 4), lax.rem(y + 3, 4)
-    vocab = tv.shape[0]
-    part = small.shape[1]
+    mine = tv.shape[0]
+    vocab = 2 * mine
+    part = fv.shape[0] * fv.shape[1]
+    width = o_ref.shape[1]
     T = res.shape[0]
     owned = part // PEERS
-    step = T // CHUNKS
+    step = T // SPANS
     per = T // 128
     R = PEERS * per
-    half, inside = me // 16, pl.multiple_of(lax.rem(me, 16) * owned, owned)
-
-    def each_peer(planes, fn):
-        planes = range(planes) if isinstance(planes, int) else planes
-
-        def chip(t, skip_self):
-            px, pz = lax.rem(x + t // 4, 4), lax.rem(zl + lax.rem(t, 4), 4)
-            for dc in range(2):
-                pc = lax.rem(core + dc, 2)
-                p = px * 8 + pz * 2 + pc
-                for k in planes:
-                    if not (skip_self and dc == 0 and k == 0):
-                        dev = {"x": px, "zl": pz, "core": pc}
-                        if k == 1:
-                            dev["zh"] = 1 - zh
-                        fn(p, k, dev)
+    chip = x * 4 + zl
+    block = core * 16 + chip
+    inside = pl.multiple_of(chip * owned, owned)
+
+    def at(px, pz, pc, plane):
+        dev = {"x": px, "zl": pz, "core": pc}
+        if plane == 1:
+            dev["zh"] = 1 - zh
+        return px * 8 + pz * 2 + pc, pc * 16 + px * 4 + pz, dev
+
+    def each_peer(fn, cores=(0, 1), plane=0, home=True):
+        if home and plane == 0:
+            fn(*at(x, zl, 1 - core, 0))
+        if home and plane == 1:
+            for pc in cores:
+                fn(*at(x, zl, pc, 1))
 
         def go(t, carry):
-            chip(t, False)
+            for pc in cores:
+                fn(*at(lax.rem(x + t // 4, 4), lax.rem(zl + lax.rem(t, 4), 4), pc, plane))
             return carry
 
         lax.fori_loop(1, 16, go, 0, unroll=UNROLL)
-        chip(0, True)
 
     bar = pltpu.get_barrier_semaphore()
 
     def greet(dev):
         pl.semaphore_signal(bar, inc=1, device_id=dev, device_id_type=MESH)
 
-    each_peer(2, lambda p, k, dev: greet(dev))
+    for plane in range(2):
+        each_peer(lambda p, b, dev: greet(dev), plane=plane)
     greet({"y": up})
     greet({"y": down})
 
     loads = [
         pltpu.make_async_copy(a, b, ld.at[i])
         for i, (a, b) in enumerate(
-            [(ids_hbm, ids_ref), (filt_hbm, fv), (table_hbm, tv), (gain_hbm, gain_ref), (taps_hbm, taps_ref), (skip_hbm, skip_ref)]
-            + [(w3_hbm.at[s, :, pl.ds(pl.multiple_of(half * 128, 128), 128)], wv.at[:, pl.ds(s * 128, 128)]) for s in range(3)]
-            + [(ct_hbm, ct_ref), (st_hbm, st_ref), (f1_hbm, f1), (w2_hbm, w2), (w2i_hbm, w2i), (f1i_hbm, f1i), (wo_hbm, wo)]
+            [
+                (ids_hbm, ids_ref),
+                (filt_hbm, fv),
+                (table_hbm.at[pl.ds(pl.multiple_of(core * mine, mine), mine)], tv),
+                (gain_hbm, gain_ref),
+                (taps_hbm, taps_ref),
+                (skip_hbm, skip_ref),
+                (w3_hbm.at[0], wv.at[:, pl.ds(0, part)]),
+                (w3_hbm.at[1], wv.at[:, pl.ds(part, part)]),
+                (w3_hbm.at[2], wv.at[:, pl.ds(2 * part, part)]),
+                (ct_hbm, ct_ref),
+                (st_hbm, st_ref),
+                (f1_hbm, f1),
+                (w2_hbm, w2),
+                (w2i_hbm, w2i),
+                (f1i_hbm, f1i),
+                (table_hbm.at[:, pl.ds(pl.multiple_of(own * width, width), width)], rt),
+                (wo_hbm.at[:, 0], wo.at[0]),
+                (wo_hbm.at[:, 1], wo.at[1]),
+            ]
         )
     ]
     for c in loads:
@@ -144,41 +164,50 @@
     idpair[...] = ids_ref[0 : per // 2, :] + ids_ref[per // 2 : per, :] * 65536
     pl.semaphore_wait(bar, 2 * PEERS + 1)
 
-    each_peer(1, lambda p, k, dev: send(idpair, idall.at[me], ids_s, ids_r, dev).start())
-    each_peer(1, lambda p, k, dev: send(fv.at[p], hx.at[me], fs, fr, dev).start())
+    each_peer(lambda p, b, dev: send(idpair, idall.at[me], ids_s, ids_r, dev).start())
+    for pc in range(2):
+        each_peer(lambda p, b, dev: send(fv.at[b], hx.at[me], fs, fr, dev).start(), cores=(pc,), home=pc == 0)
 
     def all_of(ref, s, r):
         most = ref.at[pl.ds(0, PEERS - 1)]
         return send(most, most, s, r, {"y": up})
 
     idall[me] = idpair[...]
-    hx[me] = fv[me]
+    hx[me] = fv[block]
     for i in range(4, 6):
         loads[i].wait()
 
     for r in range(3):
         for s in range(3):
-            row = jnp.where(half == 0, taps_ref[r, s : s + 1, 0:128], taps_ref[r, s : s + 1, 128:256])
+            row = jnp.where(core == 0, taps_ref[r, s : s + 1, 0:128], taps_ref[r, s : s + 1, 128:256])
             column[...] = upright(row)
             rows_t[r * 3 + s] = column[pl.ds(inside, owned), :]
-    column[...] = upright(jnp.where(half == 0, skip_ref[0:1, :], skip_ref[1:2, :]))
+    column[...] = upright(jnp.where(core == 0, skip_ref[0:1, :], skip_ref[1:2, :]))
     rows_t[9] = column[pl.ds(inside, owned), :]
     for i in range(2, 4):
         loads[i].wait()
-    normalize(tv, gain_ref, nv, 0, vocab // 32)
+    normalize(tv, gain_ref, nv, 0, mine // 32)
     for s in range(3):
         loads[6 + s].wait()
-    table_rows = []
-    for n0, n1 in ((0, 256), (256, 384)):
-        projected = dot(nv[...], wv[:, n0:n1]).astype(jnp.bfloat16).astype(jnp.float32)
-        for n in range(n0, n1, 128):
-            for v in range(vocab // 128):
-                flat[v * 128 : (v + 1) * 128, :] = jnp.transpose(projected[v * 128 : (v + 1) * 128, n - n0 : n - n0 + 128])
-            table_rows.append([flat[pl.ds(pl.multiple_of(v * 128 + inside, owned), owned), :] for v in range(vocab // 128)])
+    for s in range(3):
+        projected = dot(nv[...], wv[:, s * part : (s + 1) * part]).astype(jnp.bfloat16).astype(jnp.float32)
+        for h in range(2):
+            for v in range(mine // 128):
+                at_ = ((s * 2 + h) * 2 + v) * 128
+                flat[at_ : at_ + 128, :] = jnp.transpose(projected[v * 128 : (v + 1) * 128, h * 128 : (h + 1) * 128])
+    for h in range(2):
+        for v in range(mine // 128):
+            rows = [flat[pl.ds(pl.multiple_of(((s * 2 + h) * 2 + v) * 128 + inside, owned), owned), :] for s in range(3)]
+            rows.append(jnp.zeros((owned, 128), jnp.float32))
+            halves[h, v] = jnp.concatenate(rows, axis=0).astype(jnp.bfloat16)
+    picks_copy = send(halves.at[1 - core], picks.at[pl.ds(2 * core, 2)], pk_s, pk_r, {"core": 1 - core})
+    picks_copy.start()
+    picks[pl.ds(2 * core, 2)] = halves[core]
     groups = vocab // 128
-    picks = jnp.concatenate([table_rows[s][v] for v in range(groups) for s in range(3)], axis=0).astype(jnp.bfloat16)
 
     all_of(idall, ids_s, ids_r).wait_recv()
+    picks_copy.wait_recv()
+    table_rows = picks[...].reshape(groups * 4 * owned, 128)
     lane = lax.broadcasted_iota(jnp.int32, (owned, 128), 1)
     token = lax.broadcasted_iota(jnp.int32, (128, 128), 0)
 
@@ -187,14 +216,14 @@
             pair = [idall[i, q % (per // 2) : q % (per // 2) + 1, :] for q in (2 * q2, 2 * q2 + 1)]
             pair = [ids & 65535 if 2 * q2 + h < per // 2 else ids >> 16 for h, ids in enumerate(pair)]
             hits = [(jnp.broadcast_to(ids & 127, (128, 128)) == token).astype(jnp.float32).astype(jnp.bfloat16) for ids in pair]
-            chosen = dot(picks, jnp.concatenate(hits, axis=1))
+            chosen = dot(table_rows, jnp.concatenate(hits, axis=1))
             for h in range(2):
                 q = 2 * q2 + h
                 group = jnp.broadcast_to(pair[h] >> 7, (owned, 128))
                 short, later = [], []
                 for s in range(3):
                     of = [
-                        chosen[(v * 3 + s) * owned : (v * 3 + s + 1) * owned, h * 128 : (h + 1) * 128] for v in range(groups)
+                        chosen[(v * 4 + s) * owned : (v * 4 + s + 1) * owned, h * 128 : (h + 1) * 128] for v in range(groups)
                     ]
                     now = of[0]
                     for v in range(1, groups):
@@ -265,84 +294,109 @@
     def cols_of(q):
         return pl.ds(q * step, step)
 
-    for q in range(CHUNKS):
-        rows = slice(q * part, (q + 1) * part)
-        gain = jnp.broadcast_to(rows_t[9][None], (PEERS, owned, 128)).reshape(part, 128)
-        skipped = (flat[rows, :] + gain * pf[rows, :]).astype(jnp.bfloat16).astype(jnp.float32)
-        gated = (qf[rows, :] * skipped).astype(jnp.bfloat16)
-        sk[:, :, q * step : (q + 1) * step] = gated.reshape(PEERS, owned, 128)
+    wide = step // 128
+    for q in range(SPANS):
+        for u in range(q * wide, (q + 1) * wide):
+            rows = slice(u * part, (u + 1) * part)
+            gain = jnp.broadcast_to(rows_t[9][None], (PEERS, owned, 128)).reshape(part, 128)
+            skipped = (flat[rows, :] + gain * pf[rows, :]).astype(jnp.bfloat16).astype(jnp.float32)
+            gated = (qf[rows, :] * skipped).astype(jnp.bfloat16)
+            sk[:, :, u * 128 : (u + 1) * 128] = gated.reshape(PEERS, owned, 128)
         for plane in range(2):
             each_peer(
-                (plane,),
-                lambda p, k, dev: send(sk.at[p, :, cols_of(q)], ret.at[k, me, :, cols_of(q)], xsnd.at[k, q], xrcv.at[k, q], dev).start(),
+                lambda p, b, dev: send(
+                    sk.at[p, :, cols_of(q)], ret.at[plane, block, :, cols_of(q)], xsnd.at[plane, q], xrcv.at[plane, core, q], dev
+                ).start(),
+                plane=plane,
             )
-        ret[0, me, :, q * step : (q + 1) * step] = sk[me, :, q * step : (q + 1) * step]
+        ret[0, block, :, q * step : (q + 1) * step] = sk[me, :, q * step : (q + 1) * step]
 
     lanes = lax.broadcasted_iota(jnp.int32, (128, 128), 1)
     for b in range(per):
         col = upright(ids_ref[b : b + 1, :])
         for j in range(vocab // 128):
             hot[b * 128 : (b + 1) * 128, j * 128 : (j + 1) * 128] = (col == lanes + 128 * j).astype(jnp.float32).astype(jnp.bfloat16)
-    width = o_ref.shape[1]
-    res[...] = dot(hot[...], tv[:, pl.ds(pl.multiple_of(own * width, width), width)]).astype(jnp.bfloat16)
-    loads[15].wait()
+    for i in range(15, 18):
+        loads[i].wait()
+    res[...] = dot(hot[...], rt[...])
 
     def slot_of(k, yy):
         return (zh if k == 0 else 1 - zh) * 4 + yy
 
-    def direct(k, c, upward):
-        here = buf.at[slot_of(k, y), cols_of(c)]
+    def direct(k, g, q, upward):
+        here = buf.at[g, slot_of(k, y), cols_of(q)]
         s, r = (us, ur) if upward else (ds, dr)
-        return send(here, here, s.at[k, c], r.at[k, c], {"y": up if upward else down})
-
-    def relay(k, c):
-        upward = (c + k) % 2 == 0
-        here = buf.at[slot_of(k, down if upward else up), cols_of(c)]
-        return send(here, here, ls.at[k, c], lr.at[k, c], {"y": up if upward else down})
-
-    def returned(k, q):
-        most = ret.at[k, pl.ds(0, PEERS - 1 + k), :, cols_of(q)]
-        return send(most, most, xsnd.at[k, q], xrcv.at[k, q], {"y": up})
-
-    def turn(k, q):
-        returned(k, q).wait_recv()
-        rows = slice(q * step, (q + 1) * step)
-        arrived = ret[k, :, :, rows].astype(jnp.float32).reshape(part, step)
-        buf[slot_of(k, y), rows, :] = jnp.transpose(arrived).astype(jnp.bfloat16)
-        direct(k, q, True).start()
-        direct(k, q, False).start()
-
-    def pass_on(k, c):
-        direct(k, c, (c + k) % 2 == 0).wait_recv()
-        relay(k, c).start()
-
-    def finish(c):
-        rows = slice(c * step, (c + 1) * step)
+        return send(here, here, s.at[k, g, q], r.at[k, g, q], {"y": up if upward else down})
+
+    def rises(k, g, q):
+        return (k + g + q) % 2 == 0
+
+    def relay(k, g, q):
+        upward = rises(k, g, q)
+        here = buf.at[g, slot_of(k, down if upward else up), cols_of(q)]
+        return send(here, here, ls.at[k, g, q], lr.at[k, g, q], {"y": up if upward else down})
+
+    def returned(k, g, q, count):
+        some = ret.at[k, pl.ds(16 * g, count), :, cols_of(q)]
+        return send(some, some, xsnd.at[k, q], xrcv.at[k, g, q], {"y": up})
+
+    def turn(k, g, q):
+        if k == 0:
+
+            @pl.when(core == g)
+            def _():
+                returned(k, g, q, 15).wait_recv()
+
+            @pl.when(core != g)
+            def _():
+                returned(k, g, q, 16).wait_recv()
+        else:
+            returned(k, g, q, 16).wait_recv()
+        for u in range(wide):
+            cols = slice(q * step + u * 128, q * step + (u + 1) * 128)
+            arrived = ret[k, 16 * g : 16 * (g + 1), :, cols].astype(jnp.float32).reshape(16 * owned, 128)
+            buf[g, slot_of(k, y), cols, :] = jnp.transpose(arrived).astype(jnp.bfloat16)
+        direct(k, g, q, True).start()
+        direct(k, g, q, False).start()
+
+    def pass_on(k, g, q):
+        direct(k, g, q, rises(k, g, q)).wait_recv()
+        relay(k, g, q).start()
+
+    def finish(g, q):
         for k in range(2):
-            direct(k, c, (c + k) % 2 == 1).wait_recv()
-            relay(k, c).wait_recv()
-        acc = res[rows, :].astype(jnp.float32)
-        for j in range(TP):
-            acc += dot(buf[j, rows, :], wo[j * part : (j + 1) * part, :])
-        o_ref[rows, :] = acc.astype(jnp.bfloat16)
-
-    for s in range(CHUNKS + 3):
+            direct(k, g, q, not rises(k, g, q)).wait_recv()
+            relay(k, g, q).wait_recv()
+        for u in range(wide):
+            rows = slice(q * step + u * 128, q * step + (u + 1) * 128)
+            left = jnp.concatenate([buf[g, j, rows, :] for j in range(TP)], axis=1)
+            total = res[rows, :] + dot(left, wo[g].reshape(TP * 16 * owned, width))
+            if g == 0:
+                res[rows, :] = total
+            else:
+                o_ref[rows, :] = total.astype(jnp.bfloat16)
+
+    chunks = [(g, q) for g in range(2) for q in range(SPANS)]
+    for s in range(len(chunks) + 3):
         for k in range(2):
-            if s < CHUNKS:
-                turn(k, s)
-            if 0 <= s - 1 < CHUNKS:
-                pass_on(k, s - 1)
-        if 0 <= s - 3 < CHUNKS:
-            finish(s - 3)
+            if s < len(chunks):
+                turn(k, *chunks[s])
+            if 0 <= s - 1 < len(chunks):
+                pass_on(k, *chunks[s - 1])
+        if 0 <= s - 3 < len(chunks):
+            finish(*chunks[s - 3])
 
     all_of(idall, ids_s, ids_r).wait_send()
     all_of(hx, fs, fr).wait_send()
-    for c in range(CHUNKS):
+    picks_copy.wait_send()
+    for q in range(SPANS):
         for k in range(2):
-            returned(k, c).wait_send()
-            direct(k, c, True).wait_send()
-            direct(k, c, False).wait_send()
-            relay(k, c).wait_send()
+            sent = sk.at[pl.ds(0, PEERS - 1 + k), :, cols_of(q)]
+            send(sent, sent, xsnd.at[k, q], xrcv.at[k, 0, q], {"y": up}).wait_send()
+            for g in range(2):
+                direct(k, g, q, True).wait_send()
+                direct(k, g, q, False).wait_send()
+                relay(k, g, q).wait_send()
 
 
 def local(token_ids, embed_table, norm_gain, w_in, short_taps, long_filter, skip_gain, w_out):
@@ -371,7 +425,7 @@
         embed_table,
         jnp.transpose(w_in, (1, 0, 2)),
         long_filter.reshape(PEERS, owned, T),
-        w_out,
+        w_out.reshape(TP, 2, part // 2, cols),
         bf(f1),
         bf(w2),
         bf(w2i),
@@ -390,11 +444,14 @@
             V(ct.shape, F),
             V(st.shape, F),
             V((PEERS, owned, T), B),
-            V((vocab, width), B),
-            V((vocab, width), B),
-            V((width, 384), B),
+            V((vocab // 2, width), B),
+            V((vocab // 2, width), B),
+            V((width, 3 * part), B),
+            V((vocab, cols), B),
+            V((2, vocab // 256, 4 * owned, 128), B),
+            V((vocab // 128, 4 * owned, 128), B),
             V((T, vocab), B),
-            V(w_out.shape, B),
+            V((2, TP, part // 2, cols), B),
             V(f1.shape, B),
             V(w2.shape, B),
             V(w2i.shape, B),
@@ -402,12 +459,11 @@
             V((per // 2, 128), jnp.int32),
             V((PEERS, per // 2, 128), jnp.int32),
             V((128, 128), F),
-            V((8, part), F),
             V((10, owned, 128), F),
             V((PEERS, owned, T), B),
             V((per * part, 128), F),
             V((per * part, 128), F),
-            V((T, cols), B),
+            V((T, cols), F),
             V((per * part, 128), F),
             V((R, owned * 128), B),
             V((2, owned * R, 256), F),
@@ -415,14 +471,16 @@
             V((2 * R, owned * 128), B),
             V((PEERS, owned, T), B),
             V((2, PEERS, owned, T), B),
-            V((TP, T, part), B),
-            dma((16,)),
+            V((2, TP, T, part // 2), B),
+            dma((18,)),
+            dma,
+            dma,
             dma,
             dma,
             dma,
             dma,
         ]
-        + [dma((2, CHUNKS))] * 8,
+        + [dma((2, SPANS))] + [dma((2, 2, SPANS))] * 7,
         compiler_params=pltpu.CompilerParams(collective_id=0, has_side_effects=True, vmem_limit_bytes=48 * 2**20),
         name="block",
     )(*(pltpu.with_memory_space_constraint(a, pltpu.HBM) for a in operands))

time: 62.8 us -> 66.7 us (1.062)
  Pallas kernels: 61.6 us -> 64.9 us
    pallas_call x1, Pallas kernels: 61.6 us -> 64.9 us  [local(): pl.pallas_call(block_kernel, out_shape=jax.ShapeDtypeStruct((T, cols), B)...]
where the time goes in v6:
time: 66.7 us; the launch traced here: 65.8 us
  Pallas kernels  64.9 us (97%)
  local copies, waits for them, and re-layouts  0.88 us (1%)
    pallas_call x1, Pallas kernels, local(): pl.pallas_call(block_kernel, out_shape=jax.ShapeDtypeStruct((T, cols), B)...  64.9 us

profile of v6, /device:TPU:8, one launch (start us, length us, event | category | flops | bytes accessed | tf_op | source)
XLA Modules:
  0.0 65.8 jit_solution(9477394142780283189)
XLA Ops:
  0.0 64.9 %block.1 = bf16[768,512]{1,0:T(8,128)(2,1)S(1)} custom-call(s32[6,128]{1,0:T(8,128)} %bitcast.10, f32[1,4096]{1,0:T(1,128)} %bitcast.9, f32[3,3,256]{2,1,0:T(4,128)} %taps_hbm.1, f32[2,128]{1,0:T(2,128)} %bitcast.11, f32[192,128]{1,0:T(8,128)} %constant.12.clone.ct_hbm, f32[192,128]{1,0:T(8,128)} %constant.13.clone.st_hbm, bf16[512,4096]{1,0:T(8,128)(2,1)} %table_hbm.1, ...), custom_call_target="tpu_custom_call" | custom-call | tf_op jit(solution)/shard_map/block/pallas_call | solution.py:434
  64.9 0.9 %copy.16 = bf16[768,512]{1,0:T(8,128)(2,1)} copy(bf16[768,512]{1,0:T(8,128)(2,1)S(1)} %block.1) | data formatting | bytes 1572864

commit v7 on v5

v7 whole, which is shorter than its diff:
```python
import functools
import math

import jax
import jax.numpy as jnp
import numpy as np
from jax import lax
from jax.experimental import pallas as pl
from jax.experimental.pallas import tpu as pltpu
from jax.sharding import Mesh
from jax.sharding import PartitionSpec as P

CTX = ("x", "zl", "core")
MESH = pl.DeviceIdType.MESH
PEERS = 32
TP = 8
norm_eps = 1e-06


@functools.lru_cache(maxsize=None)
def tables(peers, per):
    R = peers * per
    N = 256 * R
    order = (np.arange(per)[:, None] + per * np.arange(peers)[None, :]).reshape(-1)
    k1 = np.arange(R) + 0.5
    a1 = 2 * np.pi * np.outer(k1, order) / (2 * R)
    f1 = np.concatenate([np.cos(a1), -np.sin(a1)], 0)
    at = 2 * np.pi * np.outer(k1, np.arange(128)) / N
    a2 = 2 * np.pi * (np.outer(np.arange(128), np.arange(128)) % 128) / 128
    c, s = np.cos(a2), np.sin(a2)
    w2 = np.block([[c, -s], [s, c]])
    w2i = np.block([[c, s], [-s, c]])
    f1i = np.concatenate([np.cos(a1.T), -np.sin(a1.T)], 1)
    return f1, np.cos(at), np.sin(at), w2, w2i, f1i


def peer_of(p):
    return {"x": p // 8, "zl": lax.rem(p // 2, 4), "core": lax.rem(p, 2)}


def ctx_index():
    return lax.axis_index("x") * 8 + lax.axis_index("zl") * 2 + lax.axis_index("core")


def dot(a, b):
    return jnp.dot(a, b, preferred_element_type=jnp.float32)


def send(src, dst, s, r, dev):
    return pltpu.make_async_remote_copy(
        src_ref=src, dst_ref=dst, send_sem=s, recv_sem=r, device_id=dev, device_id_type=MESH
    )


CHUNKS = 6
AHEAD = 3
CROSS = (2, 3)
UNROLL = 3


def normalize(tv, gain_ref, nv, first, last):
    width = tv.shape[1]

    @pl.loop(first, last)
    def _(r):
        rows = pl.ds(pl.multiple_of(r * 32, 32), 32)
        acc = jnp.zeros((32, 128), jnp.float32)
        for j in range(width // 128):
            x = tv[rows, j * 128 : (j + 1) * 128].astype(jnp.float32)
            acc += x * x
        scale = lax.rsqrt(jnp.sum(acc, axis=1, keepdims=True) * (1.0 / width) + norm_eps)
        for j in range(width // 128):
            cols = slice(j * 128, (j + 1) * 128)
            x = tv[rows, cols].astype(jnp.float32)
            nv[rows, cols] = (x * scale * gain_ref[:, cols]).astype(jnp.bfloat16)


def upright(row):
    return jnp.transpose(jnp.broadcast_to(row, (128, 128)))


def low_high(a, b):
    axis = a.ndim - 2
    first = lax.broadcasted_iota(jnp.int32, a.shape, axis) < 4
    return jnp.where(first, a, pltpu.roll(b, 4, axis)), jnp.where(first, pltpu.roll(a, 4, axis), b)


def block_kernel(
    ids_hbm, gain_hbm, taps_hbm, skip_hbm, ct_hbm, st_hbm, table_hbm, w3_hbm, filt_hbm, wo_hbm, f1_hbm, w2_hbm, w2i_hbm, f1i_hbm,
    o_ref,
    ids_ref, gain_ref, taps_ref, skip_ref, ct_ref, st_ref, fv, fsend, tv, nv, wv, rt, halves, picks, hot, wo, f1, w2, w2i, f1i,
    idpair, idall, column, rows_t, hx, pf, qf, res, flat, xs, spec, back, bs, sk, ret, buf,
    ld, ids_s, ids_r, fs, fr, pk_s, pk_r, xsnd, xrcv, zs, us, ur, ds, dr, ls, lr,
):
    x, zl, core = lax.axis_index("x"), lax.axis_index("zl"), lax.axis_index("core")
    me = ctx_index()
    zh, y = lax.axis_index("zh"), lax.axis_index("y")
    own = zh * 4 + y
    up, down = lax.rem(y + 1, 4), lax.rem(y + 3, 4)
    mine = tv.shape[0]
    vocab = 2 * mine
    owned = fv.shape[1]
    few = owned // 2
    part = PEERS * owned
    T = res.shape[0]
    width = o_ref.shape[1]
    per = T // 128
    spans = per // 2
    R = PEERS * per
    half = me // 16
    pair = pl.multiple_of(lax.rem(me, 16) // 2 * owned, owned)

    def owned_rows(ref, base):
        return low_high(
            ref[pl.ds(pl.multiple_of(base + pair, owned), owned), :], ref[pl.ds(pl.multiple_of(base + 64 + pair, owned), owned), :]
        )

    def each_peer(planes, fn):
        planes = range(planes) if isinstance(planes, int) else planes

        def chip(t, skip_self):
            px, pz = lax.rem(x + t // 4, 4), lax.rem(zl + lax.rem(t, 4), 4)
            for dc in range(2):
                pc = lax.rem(core + dc, 2)
                p = px * 8 + pz * 2 + pc
                for k in planes:
                    if not (skip_self and dc == 0 and k == 0):
                        dev = {"x": px, "zl": pz, "core": pc}
                        if k == 1:
                            dev["zh"] = 1 - zh
                        fn(p, k, dev)

        def go(t, carry):
            chip(t, False)
            return carry

        lax.fori_loop(1, 16, go, 0, unroll=UNROLL)
        chip(0, True)

    bar = pltpu.get_barrier_semaphore()

    def greet(dev):
        pl.semaphore_signal(bar, inc=1, device_id=dev, device_id_type=MESH)

    each_peer(2, lambda p, k, dev: greet(dev))
    greet({"y": up})
    greet({"y": down})

    pairs = (
        [
            (ids_hbm, ids_ref),
            (filt_hbm, fv),
            (table_hbm.at[pl.ds(pl.multiple_of(core * mine, mine), mine)], tv),
            (gain_hbm, gain_ref),
            (taps_hbm, taps_ref),
            (skip_hbm, skip_ref),
        ]
        + [(w3_hbm.at[s, :, pl.ds(pl.multiple_of(half * 128, 128), 128)], wv.at[:, pl.ds(s * 128, 128)]) for s in range(3)]
        + [
            (ct_hbm, ct_ref),
            (st_hbm, st_ref),
            (f1_hbm, f1),
            (w2_hbm, w2),
            (w2i_hbm, w2i),
            (f1i_hbm, f1i),
            (table_hbm.at[:, pl.ds(pl.multiple_of(own * width, width), width)], rt),
        ]
        + [(wo_hbm.at[:, a, h], wo.at[h, :, pl.ds(64 * a, 64)]) for a in range(2) for h in range(2)]
    )
    loads = [pltpu.make_async_copy(a, b, ld.at[i]) for i, (a, b) in enumerate(pairs)]
    for c in loads:
        c.start()
    for i in range(2):
        loads[i].wait()
    idpair[...] = ids_ref[0:spans, :] + ids_ref[spans:per, :] * 65536
    for h in range(2):
        for a in range(2):
            t0 = a * 16 + h * 8
            tiles = fv[t0 : t0 + 8].astype(jnp.float32)
            even, odd = low_high(tiles[:, :, : T // 2], tiles[:, :, T // 2 :])
            fsend[h, a * 16 : (a + 1) * 16] = jnp.stack([even, odd], axis=1).reshape(16, owned, T // 2).astype(jnp.bfloat16)
    pl.semaphore_wait(bar, 2 * PEERS + 1)

    each_peer(1, lambda p, k, dev: send(idpair, idall.at[me], ids_s, ids_r, dev).start())
    for h in range(2):
        each_peer(1, lambda p, k, dev: send(fsend.at[h, p], hx.at[h, me], fs.at[h], fr.at[h], dev).start())

    def all_of(ref, s, r):
        most = ref.at[pl.ds(0, PEERS - 1)]
        return send(most, most, s, r, {"y": up})

    idall[me] = idpair[...]
    for h in range(2):
        hx[h, me] = fsend[h, me]

    for i in range(2, 4):
        loads[i].wait()
    normalize(tv, gain_ref, nv, 0, mine // 32)
    for s in range(3):
        loads[6 + s].wait()
    for n0, n1 in ((0, 256), (256, 384)):
        projected = dot(nv[...], wv[:, n0:n1]).astype(jnp.bfloat16).astype(jnp.float32)
        for n in range(n0, n1, 128):
            for v in range(mine // 128):
                row = (n // 128 * 2 + v) * 128
                flat[row : row + 128, :] = jnp.transpose(projected[v * 128 : (v + 1) * 128, n - n0 : n - n0 + 128])
    for v in range(mine // 128):
        found = [owned_rows(flat, (s * 2 + v) * 128) for s in range(3)]
        for c in range(2):
            rows = [f[c] for f in found] + [jnp.zeros((owned, 128), jnp.float32)]
            halves[c, v] = jnp.concatenate(rows, axis=0).astype(jnp.bfloat16)
    groups = vocab // 128
    picks_copy = send(halves.at[1 - core], picks.at[pl.ds(2 * core, 2)], pk_s, pk_r, {"core": 1 - core})
    picks_copy.start()
    picks[pl.ds(2 * core, 2)] = halves[core]

    for i in range(4, 6):
        loads[i].wait()

    def own_column(row_a, row_b, to):
        column[...] = upright(jnp.where(half == 0, row_a, row_b))
        low, high = owned_rows(column, 0)
        rows_t[to] = jnp.where(core == 0, low, high)

    for r in range(3):
        for s in range(3):
            own_column(taps_ref[r, s : s + 1, 0:128], taps_ref[r, s : s + 1, 128:256], r * 3 + s)
    own_column(skip_ref[0:1, :], skip_ref[1:2, :], 9)

    all_of(idall, ids_s, ids_r).wait_recv()
    picks_copy.wait_recv()
    table_rows = picks[...].reshape(groups * 4 * owned, 128)
    lane = lax.broadcasted_iota(jnp.int32, (owned, 128), 1)
    token = lax.broadcasted_iota(jnp.int32, (128, 128), 0)

    def positions(i, carry):
        products, queries = [], []
        for q2 in range(per // 2):
            both = [idall[i, q % spans : q % spans + 1, :] for q in (2 * q2, 2 * q2 + 1)]
            both = [ids & 65535 if 2 * q2 + h < spans else ids >> 16 for h, ids in enumerate(both)]
            hits = [(jnp.broadcast_to(ids & 127, (128, 128)) == token).astype(jnp.float32).astype(jnp.bfloat16) for ids in both]
            chosen = dot(table_rows, jnp.concatenate(hits, axis=1))
            for h in range(2):
                group = jnp.broadcast_to(both[h] >> 7, (owned, 128))
                short, later = [], []
                for s in range(3):
                    of = [
                        chosen[(v * 4 + s) * owned : (v * 4 + s + 1) * owned, h * 128 : (h + 1) * 128] for v in range(groups)
                    ]
                    now = of[0]
                    for v in range(1, groups):
                        now = jnp.where(group == v, of[v], now)
                    by1, by2 = pltpu.roll(now, 1, 1), pltpu.roll(now, 2, 1)
                    before1, before2 = carry[s]
                    one = jnp.where(lane < 1, before1, by1)
                    two = jnp.where(lane < 2, before2, by2)
                    short.append(
                        (rows_t[s] * now + rows_t[3 + s] * one + rows_t[6 + s] * two).astype(jnp.bfloat16).astype(jnp.float32)
                    )
                    later.append((by1, by2))
                carry = tuple(later)
                products.append((short[1] * short[2]).astype(jnp.bfloat16).astype(jnp.float32))
                queries.append(short[0])
        for u in range(spans):
            rows = pl.ds(pl.multiple_of(u * part + i * owned, owned), owned)
            pf[0, rows, :], pf[1, rows, :] = low_high(products[u], products[u + spans])
            qf[0, rows, :], qf[1, rows, :] = low_high(queries[u], queries[u + spans])
        return carry

    nothing = jnp.zeros((owned, 128), jnp.float32)
    lax.fori_loop(0, PEERS, positions, ((nothing, nothing),) * 3, unroll=4)

    def lines(c, q):
        return pl.ds(q % spans * part + c + few * (q // spans), PEERS, stride=owned)

    def forward(src, slot):
        for c in range(few):
            for q in range(per):
                xs[q * PEERS : (q + 1) * PEERS, c * 128 : (c + 1) * 128] = src[lines(c, q), :].astype(jnp.bfloat16)
        ct, st = ct_ref[...], st_ref[...]
        for c2 in range(few // 2):
            first = dot(f1[...], xs[:, c2 * 256 : (c2 + 1) * 256])
            for h in range(2):
                c = 2 * c2 + h
                re = first[:R, h * 128 : h * 128 + 128]
                im = first[R:, h * 128 : h * 128 + 128]
                rows = slice(c * R, (c + 1) * R)
                back[rows, 0:128] = (re * ct + im * st).astype(jnp.bfloat16)
                back[rows, 128:256] = (im * ct - re * st).astype(jnp.bfloat16)
        for c in range(few):
            rows = slice(c * R, (c + 1) * R)
            spec[slot, rows, :] = dot(back[rows, :], w2[...])

    def convolve(half_index, slot):
        for u in range(spans):
            flat[u * part : (u + 1) * part, :] = (
                hx[half_index, :, :, u * 128 : (u + 1) * 128].astype(jnp.float32).reshape(part, 128)
            )
        forward(flat, 2)
        ct, st = ct_ref[...], st_ref[...]
        for c in range(few):
            rows = slice(c * R, (c + 1) * R)
            ar, ai = spec[slot, rows, 0:128], spec[slot, rows, 128:256]
            br, bi = spec[2, rows, 0:128], spec[2, rows, 128:256]
            back[rows, 0:128] = (ar * br - ai * bi).astype(jnp.bfloat16)
            back[rows, 128:256] = (ar * bi + ai * br).astype(jnp.bfloat16)
            u = dot(back[rows, :], w2i[...])
            ur_, ui_ = u[:, 0:128], u[:, 128:256]
            bs[0:R, c * 128 : (c + 1) * 128] = (ur_ * ct - ui_ * st).astype(jnp.bfloat16)
            bs[R : 2 * R, c * 128 : (c + 1) * 128] = (ui_ * ct + ur_ * st).astype(jnp.bfloat16)
        scale = 2.0 / (256 * R)
        for c2 in range(few // 2):
            z = dot(f1i[...], bs[:, c2 * 256 : (c2 + 1) * 256]) * scale
            for h in range(2):
                for q in range(per):
                    flat[lines(2 * c2 + h, q), :] = z[q * PEERS : (q + 1) * PEERS, h * 128 : h * 128 + 128]
        gain = low_high(rows_t[9], rows_t[9])[half_index]
        gain = jnp.broadcast_to(gain[None], (PEERS, owned, 128)).reshape(part, 128)
        for u in range(spans):
            rows = slice(u * part, (u + 1) * part)
            skipped = (flat[rows, :] + gain * pf[half_index, rows, :]).astype(jnp.bfloat16).astype(jnp.float32)
            gated = (qf[half_index, rows, :] * skipped).astype(jnp.bfloat16)
            sk[half_index, :, :, u * 128 : (u + 1) * 128] = gated.reshape(PEERS, owned, 128)
        ret[half_index, 0, me] = sk[half_index, me]

    chunks = [(h, u) for h in range(2) for u in range(spans)]

    def emit(c):
        h, u = chunks[c]
        cols = pl.ds(u * 128, 128)
        for plane in range(2):
            each_peer(
                (plane,),
                lambda p, k, dev: send(sk.at[h, p, :, cols], ret.at[h, k, me, :, cols], xsnd.at[k, c], xrcv.at[k, c], dev).start(),
            )

    for i in range(9, 16):
        loads[i].wait()
    forward(pf.at[0], 0)
    all_of(hx.at[0], fs.at[0], fr.at[0]).wait_recv()
    convolve(0, 0)
    for c in range(spans):
        emit(c)
    forward(pf.at[1], 1)
    lanes = lax.broadcasted_iota(jnp.int32, (128, 128), 1)
    for b in range(per):
        col = upright(ids_ref[b : b + 1, :])
        for j in range(vocab // 128):
            hot[b * 128 : (b + 1) * 128, j * 128 : (j + 1) * 128] = (col == lanes + 128 * j).astype(jnp.float32).astype(jnp.bfloat16)
    res[...] = dot(hot[...], rt[...])
    all_of(hx.at[1], fs.at[1], fr.at[1]).wait_recv()
    convolve(1, 1)

    def slot_of(k, yy):
        return (zh if k == 0 else 1 - zh) * 4 + yy

    def piece(c, slot):
        h, u = chunks[c]
        return buf.at[h, slot, u]

    def direct(k, c, upward):
        here = piece(c, slot_of(k, y))
        s, r = (us, ur) if upward else (ds, dr)
        return send(here, here, s.at[k, c], r.at[k, c], {"y": up if upward else down})

    def relay(k, c):
        if k == 1 and c in CROSS:
            here = piece(c, slot_of(0, lax.rem(y + 2, 4)))
            return send(here, here, ls.at[k, c], lr.at[k, c], {"zh": 1 - zh})
        upward = (c + k) % 2 == 0
        here = piece(c, slot_of(k, down if upward else up))
        return send(here, here, ls.at[k, c], lr.at[k, c], {"y": up if upward else down})

    def returned(k, c):
        h, u = chunks[c]
        most = ret.at[h, k, pl.ds(0, PEERS - 1 + k), :, pl.ds(u * 128, 128)]
        return send(most, most, xsnd.at[k, c], xrcv.at[k, c], {"y": up})

    def turn(k, c):
        h, u = chunks[c]
        returned(k, c).wait_recv()
        tiles = ret[h, k, :, :, u * 128 : (u + 1) * 128].astype(jnp.float32).reshape(PEERS // 2, 2, owned, 128)
        for b, rows in enumerate(low_high(tiles[:, 0], tiles[:, 1])):
            buf[h, slot_of(k, y), u, b * 128 : (b + 1) * 128, :] = jnp.transpose(rows.reshape(128, 128)).astype(jnp.bfloat16)
        direct(k, c, True).start()
        direct(k, c, False).start()

    def pass_on(k, c):
        if k == 1 and c in CROSS:
            relay(0, c).wait_recv()
        else:
            direct(k, c, (c + k) % 2 == 0).wait_recv()
        relay(k, c).start()

    def finish(c):
        h, u = chunks[c]
        for k in range(2):
            direct(k, c, (c + k) % 2 == 1).wait_recv()
            if k == 1 and c in CROSS:
                direct(k, c, (c + k) % 2 == 0).wait_recv()
            if not (k == 0 and c in CROSS):
                relay(k, c).wait_recv()
        for b in range(2):
            q = u + b * spans
            rows = slice(q * 128, (q + 1) * 128)
            left = jnp.concatenate([buf[h, j, u, b * 128 : (b + 1) * 128, :] for j in range(TP)], axis=1)
            total = res[rows, :] + dot(left, wo[h].reshape(TP * 128, width))
            if h == 0:
                res[rows, :] = total
            else:
                o_ref[rows, :] = total.astype(jnp.bfloat16)

    for i in range(16, 20):
        loads[i].wait()
    for s in range(CHUNKS + 3):
        for k in range(2):
            if s < CHUNKS:
                turn(k, s)
            if 0 <= s - 1 < CHUNKS and not (k == 1 and s - 1 in CROSS):
                pass_on(k, s - 1)
        if s + AHEAD < CHUNKS:
            emit(s + AHEAD)
        if s - 2 in CROSS:
            pass_on(1, s - 2)
        if 0 <= s - 3 < CHUNKS:
            finish(s - 3)

    all_of(idall, ids_s, ids_r).wait_send()
    picks_copy.wait_send()
    for h in range(2):
        all_of(hx.at[h], fs.at[h], fr.at[h]).wait_send()
    for c in range(CHUNKS):
        for k in range(2):
            returned(k, c).wait_send()
            direct(k, c, True).wait_send()
            direct(k, c, False).wait_send()
            relay(k, c).wait_send()


def local(token_ids, embed_table, norm_gain, w_in, short_taps, long_filter, skip_gain, w_out):
    vocab, width = embed_table.shape
    T = token_ids.shape[0]
    part = w_in.shape[2]
    owned = part // PEERS
    per = T // 128
    R = PEERS * per
    cols = w_out.shape[1]
    f1, ct, st, w2, w2i, f1i = tables(PEERS, per)
    bf = lambda a: jnp.asarray(a.astype(jnp.bfloat16))
    f32 = lambda a: jnp.asarray(a.astype(np.float32))
    vmem = pl.BlockSpec(memory_space=pltpu.VMEM)
    hbm = pl.BlockSpec(memory_space=pltpu.HBM)
    dma = pltpu.SemaphoreType.DMA
    B, F = jnp.bfloat16, jnp.float32
    V = pltpu.VMEM
    operands = (
        token_ids.reshape(per, 128),
        norm_gain.reshape(1, width),
        short_taps,
        skip_gain.reshape(part // 128, 128),
        f32(ct),
        f32(st),
        embed_table,
        jnp.transpose(w_in, (1, 0, 2)),
        long_filter.reshape(PEERS, owned, T),
        w_out.reshape(TP, 2, 2, part // 4, cols),
        bf(f1),
        bf(w2),
        bf(w2i),
        bf(f1i),
    )
    return pl.pallas_call(
        block_kernel,
        out_shape=jax.ShapeDtypeStruct((T, cols), B),
        in_specs=[hbm] * 14,
        out_specs=vmem,
        scratch_shapes=[
            V((per, 128), jnp.int32),
            V((1, width), F),
            V(short_taps.shape, F),
            V((part // 128, 128), F),
            V(ct.shape, F),
            V(st.shape, F),
            V((PEERS, owned, T), B),
            V((2, PEERS, owned, T // 2), B),
            V((vocab // 2, width), B),
            V((vocab // 2, width), B),
            V((width, 384), B),
            V((vocab, cols), B),
            V((2, vocab // 256, 4 * owned, 128), B),
            V((vocab // 128, 4 * owned, 128), B),
            V((T, vocab), B),
            V((2, TP, part // 2, cols), B),
            V(f1.shape, B),
            V(w2.shape, B),
            V(w2i.shape, B),
            V(f1i.shape, B),
            V((per // 2, 128), jnp.int32),
            V((PEERS, per // 2, 128), jnp.int32),
            V((128, 128), F),
            V((10, owned, 128), F),
            V((2, PEERS, owned, T // 2), B),
            V((2, per // 2 * part, 128), F),
            V((2, per // 2 * part, 128), F),
            V((T, cols), F),
            V((per // 2 * part, 128), F),
            V((R, owned // 2 * 128), B),
            V((3, owned // 2 * R, 256), F),
            V((owned // 2 * R, 256), B),
            V((2 * R, owned // 2 * 128), B),
            V((2, PEERS, owned, T // 2), B),
            V((2, 2, PEERS, owned, T // 2), B),
            V((2, TP, per // 2, 256, part // 2), B),
            dma((20,)),
            dma,
            dma,
            dma((2,)),
            dma((2,)),
            dma,
            dma,
        ]
        + [dma((2, CHUNKS))] * 9,
        compiler_params=pltpu.CompilerParams(collective_id=0, has_side_effects=True, vmem_limit_bytes=48 * 2**20),
        name="block",
    )(*(pltpu.with_memory_space_constraint(a, pltpu.HBM) for a in operands))


def solution(mesh):
    finer = Mesh(mesh.devices.reshape(4, 4, 2, 2, 4), ("x", "zl", "core", "zh", "y"))
    tp = ("zh", "y")
    in_specs = (
        P(CTX),
        P(),
        P(),
        P(None, None, tp),
        P(None, None, tp),
        P(tp, CTX),
        P(tp),
        P(None, tp),
    )
    return jax.shard_map(local, mesh=finer, in_specs=in_specs, out_specs=P(CTX, tp), check_vma=False)
```

time: 62.8 us -> 59.8 us (0.952)
  Pallas kernels: 61.6 us -> 58.6 us
    pallas_call x1, Pallas kernels: 61.6 us -> 58.6 us  [local(): pl.pallas_call(block_kernel, out_shape=jax.ShapeDtypeStruct((T, cols), B)...]
where the time goes in v7:
time: 59.8 us; the launch traced here: 59.5 us
  Pallas kernels  58.6 us (98%)
  local copies, waits for them, and re-layouts  0.88 us (1%)
    pallas_call x1, Pallas kernels, local(): pl.pallas_call(block_kernel, out_shape=jax.ShapeDtypeStruct((T, cols), B)...  58.6 us

profile of v7, /device:TPU:8, one launch (start us, length us, event | category | flops | bytes accessed | tf_op | source)
XLA Modules:
  0.0 59.5 jit_solution(15162505686539154821)
XLA Ops:
  0.0 58.6 %block.1 = bf16[768,512]{1,0:T(8,128)(2,1)S(1)} custom-call(s32[6,128]{1,0:T(8,128)} %bitcast.10, f32[1,4096]{1,0:T(1,128)} %bitcast.9, f32[3,3,256]{2,1,0:T(4,128)} %taps_hbm.1, f32[2,128]{1,0:T(2,128)} %bitcast.11, f32[192,128]{1,0:T(8,128)} %constant.12.clone.ct_hbm, f32[192,128]{1,0:T(8,128)} %constant.13.clone.st_hbm, bf16[512,4096]{1,0:T(8,128)(2,1)} %table_hbm.1, ...), custom_call_target="tpu_custom_call" | custom-call | tf_op jit(solution)/shard_map/block/pallas_call | solution.py:472
  58.6 0.9 %copy.16 = bf16[768,512]{1,0:T(8,128)(2,1)} copy(bf16[768,512]{1,0:T(8,128)(2,1)S(1)} %block.1) | data formatting | bytes 1572864

commit v8 on v7

--- a/solution.py
+++ b/solution.py
@@ -61,7 +61,7 @@
 def normalize(tv, gain_ref, nv, first, last):
     width = tv.shape[1]
 
-    @pl.loop(first, last)
+    @pl.loop(first, last, unroll=2)
     def _(r):
         rows = pl.ds(pl.multiple_of(r * 32, 32), 32)
         acc = jnp.zeros((32, 128), jnp.float32)
@@ -90,7 +90,7 @@
     o_ref,
     ids_ref, gain_ref, taps_ref, skip_ref, ct_ref, st_ref, fv, fsend, tv, nv, wv, rt, halves, picks, hot, wo, f1, w2, w2i, f1i,
     idpair, idall, column, rows_t, hx, pf, qf, res, flat, xs, spec, back, bs, sk, ret, buf,
-    ld, ids_s, ids_r, fs, fr, pk_s, pk_r, xsnd, xrcv, zs, us, ur, ds, dr, ls, lr,
+    ld, ids_s, ids_r, fs, fr, pk_s, pk_r, xsnd, xrcv, us, ur, ds, dr, ls, lr,
 ):
     x, zl, core = lax.axis_index("x"), lax.axis_index("zl"), lax.axis_index("core")
     me = ctx_index()
@@ -182,8 +182,11 @@
     pl.semaphore_wait(bar, 2 * PEERS + 1)
 
     each_peer(1, lambda p, k, dev: send(idpair, idall.at[me], ids_s, ids_r, dev).start())
-    for h in range(2):
+
+    def send_filter(h):
         each_peer(1, lambda p, k, dev: send(fsend.at[h, p], hx.at[h, me], fs.at[h], fr.at[h], dev).start())
+
+    send_filter(0)
 
     def all_of(ref, s, r):
         most = ref.at[pl.ds(0, PEERS - 1)]
@@ -228,8 +231,9 @@
     own_column(skip_ref[0:1, :], skip_ref[1:2, :], 9)
 
     all_of(idall, ids_s, ids_r).wait_recv()
+    send_filter(1)
     picks_copy.wait_recv()
-    table_rows = picks[...].reshape(groups * 4 * owned, 128)
+    table_rows = picks[...].astype(jnp.float32)[:, : 3 * owned, :].reshape(groups * 3 * owned, 128).astype(jnp.bfloat16)
     lane = lax.broadcasted_iota(jnp.int32, (owned, 128), 1)
     token = lax.broadcasted_iota(jnp.int32, (128, 128), 0)
 
@@ -245,7 +249,7 @@
                 short, later = [], []
                 for s in range(3):
                     of = [
-                        chosen[(v * 4 + s) * owned : (v * 4 + s + 1) * owned, h * 128 : (h + 1) * 128] for v in range(groups)
+                        chosen[(v * 3 + s) * owned : (v * 3 + s + 1) * owned, h * 128 : (h + 1) * 128] for v in range(groups)
                     ]
                     now = of[0]
                     for v in range(1, groups):
@@ -268,7 +272,7 @@
         return carry
 
     nothing = jnp.zeros((owned, 128), jnp.float32)
-    lax.fori_loop(0, PEERS, positions, ((nothing, nothing),) * 3, unroll=4)
+    lax.fori_loop(0, PEERS, positions, ((nothing, nothing),) * 3, unroll=8)
 
     def lines(c, q):
         return pl.ds(q % spans * part + c + few * (q // spans), PEERS, stride=owned)
@@ -339,8 +343,7 @@
     forward(pf.at[0], 0)
     all_of(hx.at[0], fs.at[0], fr.at[0]).wait_recv()
     convolve(0, 0)
-    for c in range(spans):
-        emit(c)
+    emit(0)
     forward(pf.at[1], 1)
     lanes = lax.broadcasted_iota(jnp.int32, (128, 128), 1)
     for b in range(per):
@@ -348,6 +351,7 @@
         for j in range(vocab // 128):
             hot[b * 128 : (b + 1) * 128, j * 128 : (j + 1) * 128] = (col == lanes + 128 * j).astype(jnp.float32).astype(jnp.bfloat16)
     res[...] = dot(hot[...], rt[...])
+    emit(1)
     all_of(hx.at[1], fs.at[1], fr.at[1]).wait_recv()
     convolve(1, 1)
 
@@ -410,6 +414,7 @@
             else:
                 o_ref[rows, :] = total.astype(jnp.bfloat16)
 
+    emit(2)
     for i in range(16, 20):
         loads[i].wait()
     for s in range(CHUNKS + 3):
@@ -519,7 +524,7 @@
             dma,
             dma,
         ]
-        + [dma((2, CHUNKS))] * 9,
+        + [dma((2, CHUNKS))] * 8,
         compiler_params=pltpu.CompilerParams(collective_id=0, has_side_effects=True, vmem_limit_bytes=48 * 2**20),
         name="block",
     )(*(pltpu.with_memory_space_constraint(a, pltpu.HBM) for a in operands))

time: 59.8 us -> 58.1 us (0.972)
  Pallas kernels: 58.6 us -> 56.7 us
    pallas_call x1, Pallas kernels: 58.6 us -> 56.7 us  [local(): pl.pallas_call(block_kernel, out_shape=jax.ShapeDtypeStruct((T, cols), B)...]
where the time goes in v8:
time: 58.1 us; the launch traced here: 57.6 us
  Pallas kernels  56.7 us (98%)
  local copies, waits for them, and re-layouts  0.88 us (2%)
    pallas_call x1, Pallas kernels, local(): pl.pallas_call(block_kernel, out_shape=jax.ShapeDtypeStruct((T, cols), B)...  56.7 us

profile of v8, /device:TPU:8, one launch (start us, length us, event | category | flops | bytes accessed | tf_op | source)
XLA Modules:
  0.0 57.6 jit_solution(14182619919347821924)
XLA Ops:
  0.0 56.7 %block.1 = bf16[768,512]{1,0:T(8,128)(2,1)S(1)} custom-call(s32[6,128]{1,0:T(8,128)} %bitcast.10, f32[1,4096]{1,0:T(1,128)} %bitcast.9, f32[3,3,256]{2,1,0:T(4,128)} %taps_hbm.1, f32[2,128]{1,0:T(2,128)} %bitcast.11, f32[192,128]{1,0:T(8,128)} %constant.12.clone.ct_hbm, f32[192,128]{1,0:T(8,128)} %constant.13.clone.st_hbm, bf16[512,4096]{1,0:T(8,128)(2,1)} %table_hbm.1, ...), custom_call_target="tpu_custom_call" | custom-call | tf_op jit(solution)/shard_map/block/pallas_call | solution.py:477
  56.7 0.9 %copy.16 = bf16[768,512]{1,0:T(8,128)(2,1)} copy(bf16[768,512]{1,0:T(8,128)(2,1)S(1)} %block.1) | data formatting | bytes 1572864

commit v9 on v8

--- a/solution.py
+++ b/solution.py
@@ -54,7 +54,7 @@
 
 CHUNKS = 6
 AHEAD = 3
-CROSS = (2, 3)
+CROSS = (1, 2)
 UNROLL = 3
 
 

time: 58.1 us -> 57.7 us (level)
  no operation moved by 1% of the time
where the time goes in v9:
time: 57.7 us; the launch traced here: 57.6 us
  Pallas kernels  56.7 us (98%)
  local copies, waits for them, and re-layouts  0.88 us (2%)
    pallas_call x1, Pallas kernels, local(): pl.pallas_call(block_kernel, out_shape=jax.ShapeDtypeStruct((T, cols), B)...  56.7 us

profile of v9, /device:TPU:8, one launch (start us, length us, event | category | flops | bytes accessed | tf_op | source)
XLA Modules:
  0.0 57.6 jit_solution(12579534243645563577)
XLA Ops:
  0.0 56.7 %block.1 = bf16[768,512]{1,0:T(8,128)(2,1)S(1)} custom-call(s32[6,128]{1,0:T(8,128)} %bitcast.10, f32[1,4096]{1,0:T(1,128)} %bitcast.9, f32[3,3,256]{2,1,0:T(4,128)} %taps_hbm.1, f32[2,128]{1,0:T(2,128)} %bitcast.11, f32[192,128]{1,0:T(8,128)} %constant.12.clone.ct_hbm, f32[192,128]{1,0:T(8,128)} %constant.13.clone.st_hbm, bf16[512,4096]{1,0:T(8,128)(2,1)} %table_hbm.1, ...), custom_call_target="tpu_custom_call" | custom-call | tf_op jit(solution)/shard_map/block/pallas_call | solution.py:477
  56.7 0.9 %copy.16 = bf16[768,512]{1,0:T(8,128)(2,1)} copy(bf16[768,512]{1,0:T(8,128)(2,1)S(1)} %block.1) | data formatting | bytes 1572864
